TPU v7x, 32 devices: a 4x4x1 block of a 4x4x8 slice. The times are simulated.
32 devices in a mesh: dp: 1 (over z), tp: 4 (over y), cp: 8 (over x, core).
Axes of the slice: x: 4, y: 4, z: 1, core: 2. Of those that a mesh axis runs over, the one named last changes fastest.
The devices are a block of a 4x4x8 slice.
Arguments:
- x: bfloat16 [2048, 3584], P(('dp', 'cp'))
- doc_id: int32 [2048], P(('dp', 'cp'))
- pos_in_doc: int32 [2048], P(('dp', 'cp'))
- norm_gain: float32 [3584], replicated
- w_q: bfloat16 [3584, 3584], P(None, 'tp')
- w_k: bfloat16 [3584, 512], P(None, 'tp')
- w_v: bfloat16 [3584, 512], P(None, 'tp')
- w_o: bfloat16 [3584, 3584], P('tp')
- inv_freq: float32 [64], replicated
Outputs:
- output 1: bfloat16 [2048, 3584], P(('dp', 'cp'))
- output 2: bfloat16 [2048, 4, 128], P(('dp', 'cp'), 'tp')
- output 3: bfloat16 [2048, 4, 128], P(('dp', 'cp'), 'tp')
All inputs are finite; a program needn't handle non-finite values.
Results may differ from a plain program's by a relative error of at most 0.00168.
Values are sent between devices in bfloat16 or wider.
A program may use at most 768 MiB of HBM per device.

v0:
```python
import jax
import jax.numpy as jnp
from jax import lax
from jax.sharding import PartitionSpec as P

QUERY_ROWS = 128


def rms_norm(x_in, norm_gain):
    x_f32 = x_in.astype(jnp.float32)
    inv_rms = lax.rsqrt(jnp.mean(x_f32 * x_f32, axis=-1, keepdims=True) + 1e-5)
    return (x_f32 * inv_rms * norm_gain).astype(jnp.bfloat16)


def apply_rope(vectors, cos_t, sin_t):
    half_dim = vectors.shape[-1] // 2
    lower_half = vectors[..., :half_dim].astype(jnp.float32)
    upper_half = vectors[..., half_dim:].astype(jnp.float32)
    turned = jnp.concatenate([lower_half * cos_t - upper_half * sin_t, upper_half * cos_t + lower_half * sin_t], axis=-1)
    return turned.astype(jnp.bfloat16)


def project(x_in, pos_in_doc, norm_gain, w_q, w_k, w_v, inv_freq):
    num_rows = x_in.shape[0]
    head_dim = 2 * inv_freq.shape[0]
    kv_heads = w_k.shape[1] // head_dim
    group_size = w_q.shape[1] // (head_dim * kv_heads)
    normed = rms_norm(x_in, norm_gain)
    q_new = jnp.dot(normed, w_q, preferred_element_type=jnp.float32).astype(jnp.bfloat16).reshape(num_rows, kv_heads, group_size, head_dim)
    k_new = jnp.dot(normed, w_k, preferred_element_type=jnp.float32).astype(jnp.bfloat16).reshape(num_rows, kv_heads, head_dim)
    v_new = jnp.dot(normed, w_v, preferred_element_type=jnp.float32).astype(jnp.bfloat16).reshape(num_rows, kv_heads, head_dim)
    rope_angle = pos_in_doc.astype(jnp.float32)[:, None] * inv_freq[None, :]
    cos_t = jnp.cos(rope_angle)
    sin_t = jnp.sin(rope_angle)
    q_rot = apply_rope(q_new, cos_t[:, None, None, :], sin_t[:, None, None, :])
    k_rot = apply_rope(k_new, cos_t[:, None, :], sin_t[:, None, :])
    return q_rot, k_rot, v_new


def global_index(stored_pos, local_rows, cp_size):
    piece_len = local_rows // 2
    owner = stored_pos // local_rows
    within = stored_pos % local_rows
    piece_id = jnp.where(within < piece_len, owner, 2 * cp_size - 1 - owner)
    return piece_id * piece_len + within % piece_len


def attention(q_rot, key_rows, val_rows, q_doc, q_idx, key_doc, key_idx):
    local_rows, kv_heads, group_size, head_dim = q_rot.shape
    blocks = local_rows // QUERY_ROWS
    score_scale = head_dim ** -0.5

    def attend(block_args):
        q_blk, doc_blk, idx_blk = block_args
        scores = jnp.einsum('qngd,knd->ngqk', q_blk, key_rows, preferred_element_type=jnp.float32) * score_scale
        visible = (doc_blk[:, None] == key_doc[None, :]) & (key_idx[None, :] <= idx_blk[:, None])
        scores = jnp.where(visible, scores, -1e30)
        attn_probs = jax.nn.softmax(scores, axis=-1).astype(jnp.bfloat16)
        return jnp.einsum('ngqk,knd->qngd', attn_probs, val_rows, preferred_element_type=jnp.float32).astype(jnp.bfloat16)

    attn_out = lax.map(attend, (q_rot.reshape(blocks, QUERY_ROWS, kv_heads, group_size, head_dim), q_doc.reshape(blocks, QUERY_ROWS), q_idx.reshape(blocks, QUERY_ROWS)))
    return attn_out.reshape(local_rows, kv_heads * group_size * head_dim)


def solution(mesh):
    cp_size = mesh.shape['cp']

    def local_step(x_in, doc_id, pos_in_doc, norm_gain, w_q, w_k, w_v, w_o, inv_freq):
        local_rows = x_in.shape[0]
        tokens = local_rows * cp_size
        q_rot, k_rot, v_new = project(x_in, pos_in_doc, norm_gain, w_q, w_k, w_v, inv_freq)
        k_all = lax.all_gather(k_rot, 'cp', tiled=True)
        v_all = lax.all_gather(v_new, 'cp', tiled=True)
        doc_all = lax.all_gather(doc_id, 'cp', tiled=True)
        cp_index = lax.axis_index('cp')
        q_idx = global_index(cp_index * local_rows + jnp.arange(local_rows), local_rows, cp_size)
        key_idx = global_index(jnp.arange(tokens), local_rows, cp_size)
        attn_out = attention(q_rot, k_all, v_all, doc_id, q_idx, doc_all, key_idx)
        part_sum = jnp.dot(attn_out, w_o, preferred_element_type=jnp.float32)
        full_sum = lax.psum(part_sum, 'tp')
        y_out = (x_in.astype(jnp.float32) + full_sum).astype(jnp.bfloat16)
        return y_out, k_rot, v_new

    row_spec = P(('dp', 'cp'))
    in_specs = (P(('dp', 'cp'), None), row_spec, row_spec, P(), P(None, 'tp'), P(None, 'tp'), P(None, 'tp'), P('tp', None), P())
    out_specs = (P(('dp', 'cp'), None), P(('dp', 'cp'), 'tp', None), P(('dp', 'cp'), 'tp', None))
    return jax.shard_map(local_step, mesh=mesh, in_specs=in_specs, out_specs=out_specs, check_vma=False)
```

profile of v0, /device:TPU:97, one launch (start us, length us, event | category | flops | bytes accessed | tf_op | source)
XLA Modules:
  0.0 212.6 jit_solution(13142463758540022085)
XLA Ops:
  7.2 0.0 copy-start
  7.2 0.1 all-reduce.2.cloned.1.call-start
  7.3 2.0 fusion.36
  9.3 0.0 copy-start.6
  9.3 0.0 copy-start.5
  9.3 6.3 %convolution_convert_fusion = bf16[256,896]{1,0:T(8,128)(2,1)} fusion(bf16[3584,896]{1,0:T(8,128)(2,1)} %param.15, bf16[256,3584]{1,0:T(8,128)(2,1)} %param.11, f32[3584]{0:T(1024)} %param.14, f32[256]{0:T(256)S(1)} %add_rsqrt_fusion), kind=kOutput, calls=%fused_computation.50 | convolution fusion | flops 1648066560 | bytes 8731648 | tf_op jit(solution)/shard_map/dot_general | solution.py:29
  15.6 0.0 copy-start.7
  15.6 1.4 copy.19
  17.0 0.0 copy-done.6
  17.0 0.0 copy-done.5
  17.0 0.3 multiply_cosine_fusion.1
  17.3 0.9 fusion.42
  18.2 1.0 concatenate.29
  19.2 1.7 concatenate.30
  20.9 1.5 pad_maximum_fusion
  22.4 1.4 copy.20
  23.8 0.0 copy-done
  23.8 0.0 copy-done.1
  23.8 0.0 copy-done.7
  23.8 0.9 fusion.40
  24.7 0.0 copy-start.4
  24.7 0.3 fusion.53
  25.0 19.4 %all_gather.10 = bf16[2048,1,128]{0,2,1:T(8,128)(2,1)} all-gather(bf16[256,1,128]{0,2,1:T(8,128)(2,1)S(1)} %pad_maximum_fusion.1), channel_id=1, replica_groups=mesh['dp'=1,'tp'=4,'cp'=8] {'cp'}, dimensions={0}, use_global_device_ids=true | all-gather | bytes 589824 | tf_op jit(solution)/shard_map/all_gather | solution.py:72
  44.4 1.3 copy.21
  45.8 1.9 convolution_convert_fusion.1
  47.7 0.0 copy-start.3
  47.7 22.2 %all-gather = bf16[2048,128]{1,0:T(8,128)(2,1)} all-gather(bf16[256,128]{1,0:T(8,128)(2,1)S(1)} %convolution_convert_fusion.1), channel_id=2, replica_groups=mesh['dp'=1,'tp'=4,'cp'=8] {'cp'}, dimensions={0}, use_global_device_ids=true | all-gather | bytes 589824 | tf_op jit(solution)/shard_map/all_gather | solution.py:73
  69.9 0.0 copy-done.4
  69.9 22.4 %all-gather.1 = s32[8,1,256]{2,1,0:T(1,128)S(1)} all-gather(s32[1,1,256]{2,1,0:T(1,128)S(1)} %bitcast.109), channel_id=1, replica_groups=mesh['dp'=1,'tp'=4,'cp'=8] {'cp'}, dimensions={0}, use_global_device_ids=true | all-gather | bytes 9216 | tf_op jit(solution)/shard_map/all_gather | solution.py:74
  92.3 0.0 copy-done.3
  92.3 15.2 %while.11 = (s32[]{:T(128)}, bf16[2,128,1,7,128]{4,1,3,2,0:T(8,128)(2,1)}, s32[2,128]{1,0:T(2,128)S(1)}, s32[2048]{0:T(1024)S(1)}, s32[2,128]{1,0:T(2,128)S(1)},...) while((s32[]{:T(128)}, ...), condition=%wide.region_4.5_spmd.clone, body=%wide.region_1.4_spmd.clone.sunk | while | flops 962500864 | bytes 26719868 | solution.py:61
  92.3 0.3 compare_and_fusion.2
  92.6 2.4 %fusion.77 = (f32[7,128]{1,0:T(8,128)S(1)}, f32[128,7,2048]{2,0,1:T(8,128)S(1)}) fusion(pred[128,2048]{1,0:T(8,128)(4,1)S(1)} %compare_and_fusion.2, bf16[2048,1,128]{2,0,1:T(8,128)(2,1)S(1)} %get-tuple-element.209, bf16[2,128,1,7,128]{4,1,3,2,0:T(8,128)(2,1)} %get-tuple-element.208, s32[]{:T(128)} %get-tuple-element.194), kind=kOutput, calls=%fused_computation.5.clone.1 | convolution fusion | flops 475266176 | bytes 8359936 | tf_op jit(solution)/shard_map/while/body/eval_jaxpr/qngd,knd->ngqk/dot_general | solution.py:55
  95.0 0.0 copy-start.2
  95.0 1.9 fusion.78
  96.9 0.0 copy-done.2
  96.9 2.9 %fusion.79 = bf16[2,128,1,7,128]{4,1,3,2,0:T(8,128)(2,1)} fusion(bf16[2,128,1,7,128]{4,1,3,2,0:T(8,128)(2,1)} %get-tuple-element.195, s32[]{:T(128)} %get-tuple-element.194, f32[7,128]{1,0:T(8,128)S(1)} %fusion.78, f32[7,128]{1,0:T(8,128)S(1)} %get-tuple-element.184, f32[128,7,2048]{2,0,1:T(8,128)S(1)} %get-tuple-element.183, ...), kind=kOutput, calls=%fused_computation.10.clone.1 | convolution fusion | flops 479051776 | bytes 8363520 | tf_op jit(solution)/shard_map/while/body/eval_jaxpr/ngqk,knd->qngd/dot_general | solution.py:59
  99.9 0.3 compare_and_fusion.2
  100.2 2.4 %fusion.77 = (f32[7,128]{1,0:T(8,128)S(1)}, f32[128,7,2048]{2,0,1:T(8,128)S(1)}) fusion(pred[128,2048]{1,0:T(8,128)(4,1)S(1)} %compare_and_fusion.2, bf16[2048,1,128]{2,0,1:T(8,128)(2,1)S(1)} %get-tuple-element.209, bf16[2,128,1,7,128]{4,1,3,2,0:T(8,128)(2,1)} %get-tuple-element.208, s32[]{:T(128)} %get-tuple-element.194), kind=kOutput, calls=%fused_computation.5.clone.1 | convolution fusion | flops 475266176 | bytes 8359936 | tf_op jit(solution)/shard_map/while/body/eval_jaxpr/qngd,knd->ngqk/dot_general | solution.py:55
  102.6 1.9 fusion.78
  104.5 0.0 copy-done.2
  104.5 2.9 %fusion.79 = bf16[2,128,1,7,128]{4,1,3,2,0:T(8,128)(2,1)} fusion(bf16[2,128,1,7,128]{4,1,3,2,0:T(8,128)(2,1)} %get-tuple-element.195, s32[]{:T(128)} %get-tuple-element.194, f32[7,128]{1,0:T(8,128)S(1)} %fusion.78, f32[7,128]{1,0:T(8,128)S(1)} %get-tuple-element.184, f32[128,7,2048]{2,0,1:T(8,128)S(1)} %get-tuple-element.183, ...), kind=kOutput, calls=%fused_computation.10.clone.1 | convolution fusion | flops 479051776 | bytes 8363520 | tf_op jit(solution)/shard_map/while/body/eval_jaxpr/ngqk,knd->qngd/dot_general | solution.py:59
  107.4 1.6 copy.22
  109.1 6.8 %fusion.45 = f32[256,3584]{1,0:T(8,128)} fusion(bf16[896,3584]{1,0:T(8,128)(2,1)} %param.18, bf16[112,8,2,128]{3,2,1,0:T(2,128)(2,1)S(1)} %bitcast.104), kind=kOutput, calls=%fused_computation.62 | convolution fusion | flops 1644167168 | bytes 10551296 | tf_op jit(solution)/shard_map/dot_general | solution.py:79
  115.8 0.1 all-reduce.2.cloned.1.call-update
  115.9 0.7 copy.23
  116.6 85.4 %all-reduce.2.cloned.1.call-done = f32[256,3584]{1,0:T(8,128)} async-done(((f32[256,3584]{1,0:T(8,128)}), f32[256,3584]{1,0:T(8,128)}) %all-reduce.2.cloned.1.call-update) | async-done | bytes 3670032 | tf_op jit(solution)/shard_map/psum | solution.py:80
  202.0 3.7 %fusion.39 = bf16[256,3584]{1,0:T(8,128)(2,1)} fusion(f32[256,3584]{1,0:T(8,128)} %all-reduce.2.cloned.1.call-done, bf16[256,3584]{1,0:T(8,128)(2,1)S(1)} %copy-done.1), kind=kLoop, calls=%fused_computation.49 | loop fusion | flops 2752512 | bytes 7340032 | tf_op jit(solution)/shard_map/convert_element_type | solution.py:81
  (11 shorter events, 0.1 us)
Async XLA Ops:
  7.2 16.6 %copy-start = (bf16[3584,128]{1,0:T(8,128)(2,1)S(1)}, bf16[3584,128]{1,0:T(8,128)(2,1)}, u32[]{:S(2)}) copy-start(bf16[3584,128]{1,0:T(8,128)(2,1)} %param.16) | copy-start | bytes 2752516
  7.2 194.8 %all-reduce.2.cloned.1.call-start = ((), (), s32[]{:S(2)}) async-start(), calls=%async_computation | async-start | bytes 7340032 | tf_op jit(solution)/shard_map/psum | solution.py:80
  9.3 7.7 %copy-start.6 = (s32[256]{0:T(256)S(1)}, s32[256]{0:T(256)}, u32[]{:S(2)}) copy-start(s32[256]{0:T(256)} %param.13) | copy-start | bytes 3076
  9.3 7.7 %copy-start.5 = (f32[64]{0:T(128)S(1)}, f32[64]{0:T(128)}, u32[]{:S(2)}) copy-start(f32[64]{0:T(128)} %param.19) | copy-start | bytes 772
  15.6 8.2 %copy-start.1 = (bf16[256,3584]{1,0:T(8,128)(2,1)S(1)}, bf16[256,3584]{1,0:T(8,128)(2,1)}, u32[]{:S(2)}) copy-start(bf16[256,3584]{1,0:T(8,128)(2,1)} %param.11) | copy-start | bytes 5505028
  15.6 8.2 %copy-start.7 = (f32[3584]{0:T(1024)S(1)}, f32[3584]{0:T(1024)}, u32[]{:S(2)}) copy-start(f32[3584]{0:T(1024)} %param.14) | copy-start | bytes 43012
  24.7 45.2 %copy-start.4 = (s32[256]{0:T(256)S(1)}, s32[256]{0:T(256)}, u32[]{:S(2)}) copy-start(s32[256]{0:T(256)} %param.12) | copy-start | bytes 3076
  47.7 44.6 %copy-start.3 = (bf16[256,128]{1,0:T(8,128)(2,1)}, bf16[256,128]{1,0:T(8,128)(2,1)S(1)}, u32[]{:S(2)}) copy-start(bf16[256,128]{1,0:T(8,128)(2,1)S(1)} %convolution_convert_fusion.1) | copy-start | bytes 196612
  95.0 1.9 copy-start.2
  102.6 1.9 copy-start.2
Sparse Core Ops, SparseCore 0:
  116.0 85.9 all-reduce.1
where the time goes:
time: 213 us
  waiting for transfers between devices  85.4 us (40%)
  blocking collectives  63.9 us (30%)
  matrix products  26.6 us (12%)
  between operations  14.2 us (7%)
  other arithmetic  13.2 us (6%)
  local copies, waits for them, and re-layouts  9.11 us (4%)
    psum x1, waiting for transfers between devices, local_step(): full_sum = lax.psum(part_sum, 'tp')  85.4 us
    all_gather x1, blocking collectives, local_step(): doc_all = lax.all_gather(doc_id, 'cp', tiled=True)  22.4 us
    all_gather x1, blocking collectives, local_step(): v_all = lax.all_gather(v_new, 'cp', tiled=True)  22.2 us
    all_gather x1, blocking collectives, local_step(): k_all = lax.all_gather(k_rot, 'cp', tiled=True)  19.4 us
    dot_general x1, matrix products, local_step(): part_sum = jnp.dot(attn_out, w_o, preferred_element_type=jnp.float32)  6.76 us
    dot_general x1, matrix products, project(): jnp.dot(normed, w_q, preferred_element_type=jnp.float32)  6.3 us
    dot_general x2, matrix products, attend(): jnp.einsum('ngqk,knd->qngd', attn_probs, val_rows, preferred_element_type...  5.86 us
    dot_general x2, matrix products, attend(): jnp.einsum('qngd,knd->ngqk', q_blk, key_rows, preferred_element_type=jnp....  4.86 us
  transfers between devices with their start and end apart: 1, of which 1 were waited for; matrix products, arithmetic and copies ran while one was open for 0% of the time, Pallas kernels for 0%

commit v1 on v0

v1 whole, which is shorter than its diff:
```python
import jax
import jax.numpy as jnp
from jax import lax
from jax.experimental import pallas as pl
from jax.experimental.pallas import tpu as pltpu
from jax.sharding import PartitionSpec as P

MESH = pl.DeviceIdType.MESH
BF16, F32 = jnp.bfloat16, jnp.float32
LOG2E = 1.4426950408889634
KEY_BLOCK = 256


class Copies:
    def __init__(self, send_sem, recv_sem):
        self.send_sem, self.recv_sem, self.used = send_sem, recv_sem, 0

    def take(self, count):
        first = self.used
        self.used += count
        return first

    def make(self, index, src, dst, device):
        return pltpu.make_async_remote_copy(
            src_ref=src, dst_ref=dst, send_sem=self.send_sem.at[index], recv_sem=self.recv_sem.at[index],
            device_id=device, device_id_type=MESH)


class RingGather:
    def __init__(self, copies, right_dev, left_dev, here, left, right, far, at_right, at_left, at_far):
        first = copies.take(6)
        self.own = {}
        self.got = {}
        for half in (0, 1):
            self.own['r', half] = copies.make(first + half, here(half), at_right(half), right_dev)
            self.own['l', half] = copies.make(first + 2 + half, here(half), at_left(half), left_dev)
            self.got['r', half] = copies.make(first + half, left(half), left(half), right_dev)
            self.got['l', half] = copies.make(first + 2 + half, right(half), right(half), left_dev)
        self.passed = (copies.make(first + 4, left(0), at_far(0), right_dev),
                       copies.make(first + 5, right(1), at_far(1), left_dev))
        self.far_got = (copies.make(first + 4, far(0), far(0), right_dev),
                        copies.make(first + 5, far(1), far(1), left_dev))

    def send(self):
        for key in (('r', 0), ('l', 1), ('r', 1), ('l', 0)):
            self.own[key].start()

    def relay(self):
        self.got['r', 0].wait_recv()
        self.passed[0].start()
        self.got['l', 1].wait_recv()
        self.passed[1].start()

    def near(self):
        self.got['r', 1].wait_recv()
        self.got['l', 0].wait_recv()

    def last(self):
        self.far_got[0].wait_recv()
        self.far_got[1].wait_recv()

    def drain(self):
        for copy in self.own.values():
            copy.wait_send()
        for copy in self.passed:
            copy.wait_send()


class ChipGather:
    def __init__(self, copies, right_dev, left_dev, sib_dev, region, own, left, right, far, other):
        def at(owner):
            return lambda half: region(owner, half)
        self.ring = RingGather(copies, right_dev, left_dev, at(own), at(left), at(right), at(far),
                               at(own), at(own), lambda half: region(left if half == 0 else right, half))
        self.out, self.back = {}, {}
        for name, owner in (('own', own), ('left', left), ('right', right), ('far', far)):
            for half in (0, 1):
                index = copies.take(1)
                self.out[name, half] = copies.make(index, region(owner, half), region(owner, half), sib_dev)
                self.back[name, half] = copies.make(index, region(other(owner), half), region(other(owner), half), sib_dev)

    def send(self):
        self.ring.send()
        self.out['own', 0].start()
        self.out['own', 1].start()

    def relay(self):
        self.ring.relay()
        self.out['left', 0].start()
        self.out['right', 1].start()

    def near(self):
        self.ring.near()
        self.out['left', 1].start()
        self.out['right', 0].start()

    def last(self):
        self.ring.last()
        self.out['far', 0].start()
        self.out['far', 1].start()

    def finish(self):
        for copy in self.back.values():
            copy.wait_recv()

    def drain(self):
        self.ring.drain()
        for copy in self.out.values():
            copy.wait_send()


def layer_kernel(tp_size, cp_size, x_hbm, pos_hbm, gain_hbm, wq_hbm, wk_hbm, wv_hbm, wo_hbm, freq_hbm,
                 y_hbm, kc_hbm, vc_hbm,
                 xv, hv, gain_v, pos_v, freq_v, wkv, wq, wo, kv, qs, cos_v, sin_v, cap_v, scores, run_max, run_sum,
                 acc, oall, yall, load_sem, store_sem, send_sem, recv_sem):
    rows, width = xv.shape
    piece = rows // 2
    head_dim = wk_hbm.shape[1]
    half_dim = head_dim // 2
    head_cols = wq_hbm.shape[1]
    heads = head_cols // head_dim
    out_cols = width // tp_size
    low_rows = piece * cp_size
    share = head_cols // cp_size
    cut = (share // 2 + 15) // 16 * 16
    score_scale = head_dim ** -0.5 * LOG2E

    t = lax.axis_index('tp')
    c = lax.axis_index('cp')
    chips = cp_size // 2
    core = lax.rem(c, 2)
    chip = c // 2

    def tp_at(step):
        return lax.rem(t + step, tp_size)

    def cp_at(step):
        return lax.rem(chip + step, chips) * 2 + core

    def other(owner):
        return owner + 1 - 2 * core

    up, down = {'tp': tp_at(1)}, {'tp': tp_at(tp_size - 1)}
    right, left, sib = {'cp': cp_at(1)}, {'cp': cp_at(chips - 1)}, {'cp': other(c)}

    loads = {}

    def load(name, src, dst):
        loads[name] = pltpu.make_async_copy(src, dst, load_sem.at[len(loads)])
        loads[name].start()

    load('pos', pos_hbm, pos_v)
    load('freq', freq_hbm, freq_v)
    load('gain', gain_hbm, gain_v)
    for p in (0, 1):
        load(('x', p), x_hbm.at[pl.ds(p * piece, piece)], xv.at[pl.ds(p * piece, piece)])
    load('wk', wk_hbm, wkv.at[:, pl.ds(0, head_dim)])
    load('wv', wv_hbm, wkv.at[:, pl.ds(head_dim, head_dim)])
    q_chunks = ((0, 4), (4, heads - 4))
    for first, count in q_chunks:
        cols = pl.ds(first * head_dim, count * head_dim)
        load(('wq', first), wq_hbm.at[:, cols], wq.at[:, cols])
    own_cols = pl.multiple_of(t * out_cols, 128)
    load('wo', wo_hbm.at[:, pl.ds(own_cols, out_cols)], wo.at[0])

    barrier = pltpu.get_barrier_semaphore()
    peers = [{'tp': tp_at(step)} for step in range(1, tp_size)] + [right, left, sib]
    for peer in peers:
        pl.semaphore_signal(barrier, inc=1, device_id=peer, device_id_type=MESH)
    pl.semaphore_wait(barrier, len(peers))

    copies = Copies(send_sem, recv_sem)

    col_chunks = ((0, 512), (512, out_cols - 512))
    share_row = pl.multiple_of(c * share, 16)
    wo_out, wo_in = {}, {}
    for n, (start, size) in enumerate(col_chunks):
        for step in range(1, tp_size):
            index = copies.take(1)
            src_col = pl.multiple_of(tp_at(step) * out_cols + start, 128)
            wo_out[n, step] = copies.make(
                index, wo_hbm.at[pl.ds(share_row, share), pl.ds(src_col, size)],
                wo.at[tp_size - step, pl.ds(share_row, share), pl.ds(start, size)], {'tp': tp_at(step)})
            wo_out[n, step].start()
            landed = wo.at[tp_size - step, pl.ds(share_row, share), pl.ds(start, size)]
            wo_in[n, step] = copies.make(index, landed, landed, {'tp': tp_at(step)})

    def wo_region(n):
        start, size = col_chunks[n]

        def region(owner, half):
            first = pl.multiple_of(owner * share + (cut if half else 0), 16)
            return wo.at[pl.ds(1, tp_size - 1), pl.ds(first, share - cut if half else cut), pl.ds(start, size)]
        return region

    def kv_region(p):
        def region(owner, half):
            return kv.at[half, pl.ds(pl.multiple_of(p * low_rows + owner * piece, piece), piece)]
        return region

    def chip_gather(region):
        return ChipGather(copies, right, left, sib, region, c, cp_at(chips - 1), cp_at(1), cp_at(2), other)

    kv_gather = [chip_gather(kv_region(p)) for p in (0, 1)]
    wo_gather = [chip_gather(wo_region(n)) for n in range(len(col_chunks))]

    def tp_gather(buf, first, count, start, size):
        def at(slot):
            def region(half):
                return buf.at[slot, pl.ds(first + half * (count // 2), count // 2), pl.ds(start, size)]
            return region
        return RingGather(copies, up, down, at(0), at(3), at(1), at(2), at(3), at(1), at(2))

    o_gather = [tp_gather(oall, p * piece, piece, 0, head_cols) for p in (0, 1)]
    y_gather = {(p, n): tp_gather(yall, p * piece, piece, start, size)
                for p in (0, 1) for n, (start, size) in enumerate(col_chunks)}

    loads['pos'].wait()
    loads['freq'].wait()
    freq = jnp.concatenate([freq_v[...], freq_v[...]], axis=-1)
    lower = lax.broadcasted_iota(jnp.int32, (piece, head_dim), 1) < half_dim

    def pos_column(p):
        pos_row = pos_v[:, pl.ds(p * piece, piece)].astype(F32)
        return jnp.transpose(jnp.broadcast_to(pos_row, (piece, piece)))

    for p in (0, 1):
        angle = pos_column(p) * freq
        sine = jnp.sin(angle)
        cos_v[pl.ds(p * piece, piece), :] = jnp.cos(angle)
        sin_v[pl.ds(p * piece, piece), :] = jnp.where(lower, -sine, sine)

    def rope(vec, p):
        vec = vec.astype(F32)
        part = pl.ds(p * piece, piece)
        return (vec * cos_v[part, :] + pltpu.roll(vec, half_dim, 1) * sin_v[part, :]).astype(BF16)

    loads['gain'].wait()
    norm_rows = 16
    for p in (0, 1):
        loads['x', p].wait()

        def norm_step(step, _, p=p):
            part = pl.ds(pl.multiple_of(p * piece + step * norm_rows, norm_rows), norm_rows)
            x_f32 = xv[part, :].astype(F32)
            inv_rms = lax.rsqrt(jnp.mean(x_f32 * x_f32, axis=-1, keepdims=True) + 1e-5)
            hv[part, :] = (x_f32 * inv_rms * gain_v[...]).astype(BF16)
            return 0
        lax.fori_loop(0, piece // norm_rows, norm_step, 0)

    loads['wk'].wait()
    loads['wv'].wait()
    kv_new = jnp.dot(hv[...], wkv[...], preferred_element_type=F32).astype(BF16)
    for p in (0, 1):
        block = kv_new[p * piece:(p + 1) * piece]
        kv_region(p)(c, 0)[...] = rope(block[:, :head_dim], p)
        kv_region(p)(c, 1)[...] = block[:, head_dim:]
        kv_gather[p].send()
    stores = []

    def store(src, dst):
        stores.append(pltpu.make_async_copy(src, dst, store_sem.at[len(stores)]))
        stores[-1].start()

    for p in (0, 1):
        store(kv_region(p)(c, 0), kc_hbm.at[pl.ds(p * piece, piece)])
        store(kv_region(p)(c, 1), vc_hbm.at[pl.ds(p * piece, piece)])

    def queries(first, count):
        loads['wq', first].wait()
        new = jnp.dot(hv[...], wq[:, pl.ds(first * head_dim, count * head_dim)], preferred_element_type=F32).astype(BF16)
        for h in range(count):
            for p in (0, 1):
                qs[p, pl.ds((first + h) * piece, piece), :] = rope(
                    new[p * piece:(p + 1) * piece, h * head_dim:(h + 1) * head_dim], p)

    queries(*q_chunks[0])
    for p in (0, 1):
        kv_gather[p].relay()
    queries(*q_chunks[1])
    for p in (0, 1):
        kv_gather[p].near()
    for p in (0, 1):
        kv_gather[p].last()

    def attend(p):
        low_blocks = (chip + 1) if p == 0 else chips
        blocks = low_blocks if p == 0 else low_blocks + chips - chip
        piece_id = c if p == 0 else 2 * cp_size - 1 - c
        pos_col = pos_column(p)
        q_idx = (piece_id * piece).astype(F32) + lax.broadcasted_iota(jnp.int32, (piece, piece), 0).astype(F32)
        doc_start = q_idx - pos_col
        lane = lax.broadcasted_iota(jnp.int32, (piece, piece), 1).astype(F32)
        run_max[...] = jnp.full(run_max.shape, -jnp.inf, F32)
        run_sum[...] = jnp.zeros(run_sum.shape, F32)

        def key_rows(step):
            block = jnp.where(step < low_blocks, step, step - low_blocks + chip + chips)
            return block, pl.ds(pl.multiple_of(block * KEY_BLOCK, KEY_BLOCK), KEY_BLOCK)

        def score_step(step, _):
            block, part = key_rows(step)
            for half in (0, 1):
                owner = block * 2 + half
                owner_piece = jnp.where(owner < cp_size, owner, 3 * cp_size - 1 - owner)
                key_idx = (owner_piece * piece).astype(F32) + lane
                seen = (key_idx >= doc_start) & (key_idx <= q_idx)
                cap_v[:, half * piece:(half + 1) * piece] = jnp.where(seen, jnp.inf, -jnp.inf)
            raw = lax.dot_general(qs[p], kv[0, part, :], (((1,), (1,)), ((), ())), preferred_element_type=F32)
            for h in range(heads):
                mine = slice(h * piece, (h + 1) * piece)
                capped = jnp.minimum(raw[mine], cap_v[...])
                scores[step, mine, :] = capped
                run_max[mine, :] = jnp.maximum(run_max[mine, :], jnp.maximum(capped[:, :piece], capped[:, piece:]))
            return 0
        lax.fori_loop(0, blocks, score_step, 0)
        for h in range(heads):
            mine = slice(h * piece, (h + 1) * piece)
            top = jnp.max(run_max[mine, :], axis=-1, keepdims=True) * score_scale
            run_max[mine, :] = jnp.broadcast_to(top, (piece, piece))

        def sum_step(step, _):
            for h in range(heads):
                mine = slice(h * piece, (h + 1) * piece)
                shift = run_max[mine, :]
                run_sum[mine, :] += (jnp.exp2(scores[step, mine, :piece] * score_scale - shift)
                                     + jnp.exp2(scores[step, mine, piece:] * score_scale - shift))
            return 0
        lax.fori_loop(0, blocks, sum_step, 0)
        for h in range(heads):
            mine = slice(h * piece, (h + 1) * piece)
            total = jnp.sum(run_sum[mine, :], axis=-1, keepdims=True)
            run_max[mine, :] = run_max[mine, :] + jnp.broadcast_to(jnp.log2(total), (piece, piece))
        acc[...] = jnp.zeros(acc.shape, F32)

        def value_step(step, _):
            _, part = key_rows(step)
            shift = run_max[...]
            probs = jnp.concatenate([jnp.exp2(scores[step, :, :piece] * score_scale - shift).astype(BF16),
                                     jnp.exp2(scores[step, :, piece:] * score_scale - shift).astype(BF16)], axis=-1)
            acc[...] += jnp.dot(probs, kv[1, part, :], preferred_element_type=F32)
            return 0
        lax.fori_loop(0, blocks, value_step, 0)
        for h in range(heads):
            oall[0, pl.ds(p * piece, piece), h * head_dim:(h + 1) * head_dim] = (
                acc[h * piece:(h + 1) * piece, :].astype(BF16))

    for step in range(1, tp_size):
        wo_in[0, step].wait_recv()
    wo_gather[0].send()
    kv_gather[0].finish()
    kv_gather[1].finish()
    attend(0)
    o_gather[0].send()
    attend(1)
    o_gather[1].send()

    wo_gather[0].relay()
    o_gather[0].relay()
    for step in range(1, tp_size):
        wo_in[1, step].wait_recv()
    wo_gather[1].send()
    wo_gather[0].near()
    o_gather[0].near()
    o_gather[1].relay()
    wo_gather[0].last()
    o_gather[0].last()
    loads['wo'].wait()
    wo_gather[0].finish()

    def project(p, n):
        start, size = col_chunks[n]
        part = pl.ds(p * piece, piece)
        total = xv[part, pl.ds(pl.multiple_of(own_cols + start, 128), size)].astype(F32)
        mixed = jnp.dot(oall[0, part, :], wo[0, :, pl.ds(start, size)], preferred_element_type=F32)
        for slot in range(1, tp_size):
            mixed = mixed + jnp.dot(oall[slot, part, :], wo[slot, :, pl.ds(start, size)], preferred_element_type=F32)
        yall[0, part, pl.ds(start, size)] = (total + mixed).astype(BF16)
        y_gather[p, n].send()

    def put(p, n):
        start, size = col_chunks[n]
        part = pl.ds(p * piece, piece)
        for slot in range(tp_size):
            store(yall.at[slot, part, pl.ds(start, size)],
                  y_hbm.at[part, pl.ds(pl.multiple_of(tp_at(slot) * out_cols + start, 128), size)])

    project(0, 0)
    o_gather[1].near()
    wo_gather[1].relay()
    o_gather[1].last()
    project(1, 0)
    y_gather[0, 0].relay()
    wo_gather[1].near()
    wo_gather[1].last()
    wo_gather[1].finish()
    project(0, 1)
    y_gather[1, 0].relay()
    project(1, 1)
    y_gather[0, 0].near()
    y_gather[0, 0].last()
    put(0, 0)
    y_gather[0, 1].relay()
    y_gather[1, 0].near()
    y_gather[1, 0].last()
    put(1, 0)
    y_gather[1, 1].relay()
    y_gather[0, 1].near()
    y_gather[0, 1].last()
    put(0, 1)
    y_gather[1, 1].near()
    y_gather[1, 1].last()
    put(1, 1)

    for copy in wo_out.values():
        copy.wait_send()
    for gather in kv_gather + wo_gather + o_gather + list(y_gather.values()):
        gather.drain()
    for copy in stores:
        copy.wait()
    assert copies.used == send_sem.shape[0]


def solution(mesh):
    tp_size, cp_size = mesh.shape['tp'], mesh.shape['cp']

    def local_step(x_in, doc_id, pos_in_doc, norm_gain, w_q, w_k, w_v, w_o, inv_freq):
        del doc_id
        rows, width = x_in.shape
        piece = rows // 2
        head_dim = w_k.shape[1]
        head_cols = w_q.shape[1]
        heads = head_cols // head_dim
        out_cols = width // tp_size
        copies = 2 * (tp_size - 1) + 4 * 14 + 6 * 6
        stack = heads * piece
        y_out, k_new, v_new = pl.pallas_call(
            lambda *refs: layer_kernel(tp_size, cp_size, *refs),
            out_shape=(jax.ShapeDtypeStruct(x_in.shape, BF16), jax.ShapeDtypeStruct((rows, head_dim), BF16),
                       jax.ShapeDtypeStruct((rows, head_dim), BF16)),
            in_specs=[pl.BlockSpec(memory_space=pl.ANY)] * 8,
            out_specs=[pl.BlockSpec(memory_space=pl.ANY)] * 3,
            scratch_shapes=[
                pltpu.VMEM((rows, width), BF16),
                pltpu.VMEM((rows, width), BF16),
                pltpu.VMEM((1, width), F32),
                pltpu.VMEM((1, rows), jnp.int32),
                pltpu.VMEM((1, head_dim // 2), F32),
                pltpu.VMEM((width, 2 * head_dim), BF16),
                pltpu.VMEM((width, head_cols), BF16),
                pltpu.VMEM((tp_size, head_cols, out_cols), BF16),
                pltpu.VMEM((2, rows * cp_size, head_dim), BF16),
                pltpu.VMEM((2, stack, head_dim), BF16),
                pltpu.VMEM((rows, head_dim), F32),
                pltpu.VMEM((rows, head_dim), F32),
                pltpu.VMEM((piece, KEY_BLOCK), F32),
                pltpu.VMEM((rows * cp_size // KEY_BLOCK, stack, KEY_BLOCK), F32),
                pltpu.VMEM((stack, piece), F32),
                pltpu.VMEM((stack, piece), F32),
                pltpu.VMEM((stack, head_dim), F32),
                pltpu.VMEM((tp_size, rows, head_cols), BF16),
                pltpu.VMEM((tp_size, rows, out_cols), BF16),
                pltpu.SemaphoreType.DMA((10,)),
                pltpu.SemaphoreType.DMA((4 + 4 * tp_size,)),
                pltpu.SemaphoreType.DMA((copies,)),
                pltpu.SemaphoreType.DMA((copies,)),
            ],
            compiler_params=pltpu.CompilerParams(
                collective_id=0, has_side_effects=True, vmem_limit_bytes=60 * 1024 * 1024),
            name='layer',
        )(x_in, pos_in_doc.reshape(1, rows), norm_gain.reshape(1, width), w_q, w_k, w_v, w_o,
          inv_freq.reshape(1, head_dim // 2))
        kv_heads = 1
        return y_out, k_new.reshape(rows, kv_heads, head_dim), v_new.reshape(rows, kv_heads, head_dim)

    row_spec = P(('dp', 'cp'))
    in_specs = (P(('dp', 'cp'), None), row_spec, row_spec, P(), P(None, 'tp'), P(None, 'tp'), P(None, 'tp'), P('tp', None), P())
    out_specs = (P(('dp', 'cp'), None), P(('dp', 'cp'), 'tp', None), P(('dp', 'cp'), 'tp', None))
    return jax.shard_map(local_step, mesh=mesh, in_specs=in_specs, out_specs=out_specs, check_vma=False)
```

time: 213 us -> 66 us (0.31)
  waiting for transfers between devices: 85.4 us -> 0 us
  blocking collectives: 63.9 us -> 0 us
  Pallas kernels: 0 us -> 59.6 us
  matrix products: 26.6 us -> 0 us
  between operations: 14.2 us -> 0.66 us
  other arithmetic: 13.2 us -> 0 us
  local copies, waits for them, and re-layouts: 9.11 us -> 5.48 us
    psum x1 -> x0, waiting for transfers between devices: 85.4 us -> none  [local_step(): full_sum = lax.psum(part_sum, 'tp')]
    all_gather x3 -> x0, blocking collectives: 63.9 us -> none  [the longest x1 22.4 us: local_step(): doc_all = lax.all_gather(doc_id, 'cp', tiled=True)]
    pallas_call x0 -> x1, Pallas kernels: none -> 59.6 us  [local_step(): pl.pallas_call(lambda *refs: layer_kernel(tp_size, cp_size, *refs), out_s...]
    dot_general x8 -> x0, matrix products: 26.6 us -> none  [the longest x1 6.76 us: local_step(): part_sum = jnp.dot(attn_out, w_o, preferred_element_type=jnp.float32)]
    reduce_sum x3 -> x0, other arithmetic: 5.79 us -> none  [the longest x2 3.78 us: attend(): attn_probs = jax.nn.softmax(scores, axis=-1).astype(jnp.bfloat16)]
    convert_element_type x2 -> x0, other arithmetic: 3.68 us -> none  [the longest x1 3.67 us: local_step(): y_out = (x_in.astype(jnp.float32) + full_sum).astype(jnp.bfloat16)]
    concatenate x2 -> x0, local copies, waits for them, and re-layouts: 2.66 us -> none  [apply_rope(): jnp.concatenate([lower_half * cos_t - upper_half * sin_t, upper_half * co...]
  transfers between devices with their start and end apart: 1 -> 0, of which waited for: 1 -> 0; matrix products, arithmetic and copies ran while one was open for 0% -> 0% of each run, Pallas kernels for 0% -> 0%
where the time goes in v1:
time: 66 us; the launch traced here: 65.8 us
  Pallas kernels  59.6 us (90%)
  local copies, waits for them, and re-layouts  5.48 us (8%)
  between operations  0.66 us (1%)
    pallas_call x1, Pallas kernels, local_step(): pl.pallas_call(lambda *refs: layer_kernel(tp_size, cp_size, *refs), out_s...  59.6 us
    unnamed x7, local copies, waits for them, and re-layouts  4.15 us
    reshape x1, local copies, waits for them, and re-layouts, local_step(): norm_gain.reshape(1, width)  1.33 us

profile of v1, /device:TPU:97, one launch (start us, length us, event | category | flops | bytes accessed | tf_op | source)
XLA Modules:
  0.0 65.8 jit_solution(14814727322725725887)
XLA Ops:
  0.6 1.3 %reshape.22.refs_2_ = f32[1,3584]{1,0:T(1,128)} reshape(f32[3584]{0:T(1024)} %param.11) | data formatting | bytes 28672 | tf_op jit(solution)/shard_map/reshape | solution.py:471
  2.0 59.6 %layer.1 = (bf16[256,3584]{1,0:T(8,128)(2,1)}, bf16[256,128]{1,0:T(8,128)(2,1)}, bf16[256,128]{1,0:T(8,128)(2,1)}) custom-call(bf16[256,3584]{1,0:T(8,128)(2,1)} %refs_0_.1, s32[1,256]{1,0:T(1,128)} %bitcast.6, f32[1,3584]{1,0:T(1,128)} %reshape.22.refs_2_, bf16[3584,896]{1,0:T(8,128)(2,1)} %refs_3_.1, bf16[3584,128]{1,0:T(8,128)(2,1)} %refs_4_.1, ...), custom_call_target="tpu_custom_call" | custom-call | tf_op jit(solution)/shard_map/layer/pallas_call | solution.py:437
  61.6 0.0 copy-start.1
  61.6 0.0 copy-start
  61.6 2.9 %copy.14 = bf16[256,3584]{1,0:T(8,128)(2,1)} copy(bf16[256,3584]{1,0:T(8,128)(2,1)} %get-tuple-element.12) | data formatting | bytes 3670016
  64.5 0.0 copy-done.1
  64.5 0.6 copy.15
  65.1 0.0 copy-done
  65.2 0.6 copy.16
Async XLA Ops:
  61.6 2.9 %copy-start.1 = (bf16[256,128]{1,0:T(8,128)(2,1)S(1)}, bf16[256,128]{1,0:T(8,128)(2,1)}, u32[]{:S(2)}) copy-start(bf16[256,128]{1,0:T(8,128)(2,1)} %get-tuple-element.7) | copy-start | bytes 196612
  61.6 3.5 %copy-start = (bf16[256,128]{1,0:T(8,128)(2,1)S(1)}, bf16[256,128]{1,0:T(8,128)(2,1)}, u32[]{:S(2)}) copy-start(bf16[256,128]{1,0:T(8,128)(2,1)} %get-tuple-element.8) | copy-start | bytes 196612

commit v2 on v1

--- a/solution.py
+++ b/solution.py
@@ -8,6 +8,7 @@
 MESH = pl.DeviceIdType.MESH
 BF16, F32 = jnp.bfloat16, jnp.float32
 LOG2E = 1.4426950408889634
+LOWEST = -1e38
 KEY_BLOCK = 256
 
 
@@ -110,9 +111,9 @@
 
 
 def layer_kernel(tp_size, cp_size, x_hbm, pos_hbm, gain_hbm, wq_hbm, wk_hbm, wv_hbm, wo_hbm, freq_hbm,
-                 y_hbm, kc_hbm, vc_hbm,
-                 xv, hv, gain_v, pos_v, freq_v, wkv, wq, wo, kv, qs, cos_v, sin_v, cap_v, scores, run_max, run_sum,
-                 acc, oall, yall, load_sem, store_sem, send_sem, recv_sem):
+                 y_out, kc_out, vc_out,
+                 xv, hv, gain_raw, gain_v, pos_v, freq_v, wkv, wq, wo, kv, qs, cos_v, sin_v, cap_v, scores, run_max,
+                 run_sum, acc, oall, load_sem, send_sem, recv_sem):
     rows, width = xv.shape
     piece = rows // 2
     head_dim = wk_hbm.shape[1]
@@ -151,23 +152,18 @@
 
     load('pos', pos_hbm, pos_v)
     load('freq', freq_hbm, freq_v)
-    load('gain', gain_hbm, gain_v)
-    for p in (0, 1):
-        load(('x', p), x_hbm.at[pl.ds(p * piece, piece)], xv.at[pl.ds(p * piece, piece)])
+    load('gain', gain_hbm, gain_raw)
+    load(('x', 0), x_hbm.at[pl.ds(0, piece)], xv.at[pl.ds(0, piece)])
     load('wk', wk_hbm, wkv.at[:, pl.ds(0, head_dim)])
     load('wv', wv_hbm, wkv.at[:, pl.ds(head_dim, head_dim)])
+    load(('x', 1), x_hbm.at[pl.ds(piece, piece)], xv.at[pl.ds(piece, piece)])
+    own_cols = pl.multiple_of(t * out_cols, 128)
     q_chunks = ((0, 4), (4, heads - 4))
-    for first, count in q_chunks:
-        cols = pl.ds(first * head_dim, count * head_dim)
-        load(('wq', first), wq_hbm.at[:, cols], wq.at[:, cols])
-    own_cols = pl.multiple_of(t * out_cols, 128)
-    load('wo', wo_hbm.at[:, pl.ds(own_cols, out_cols)], wo.at[0])
 
     barrier = pltpu.get_barrier_semaphore()
     peers = [{'tp': tp_at(step)} for step in range(1, tp_size)] + [right, left, sib]
     for peer in peers:
         pl.semaphore_signal(barrier, inc=1, device_id=peer, device_id_type=MESH)
-    pl.semaphore_wait(barrier, len(peers))
 
     copies = Copies(send_sem, recv_sem)
 
@@ -181,7 +177,6 @@
             wo_out[n, step] = copies.make(
                 index, wo_hbm.at[pl.ds(share_row, share), pl.ds(src_col, size)],
                 wo.at[tp_size - step, pl.ds(share_row, share), pl.ds(start, size)], {'tp': tp_at(step)})
-            wo_out[n, step].start()
             landed = wo.at[tp_size - step, pl.ds(share_row, share), pl.ds(start, size)]
             wo_in[n, step] = copies.make(index, landed, landed, {'tp': tp_at(step)})
 
@@ -204,16 +199,24 @@
     kv_gather = [chip_gather(kv_region(p)) for p in (0, 1)]
     wo_gather = [chip_gather(wo_region(n)) for n in range(len(col_chunks))]
 
-    def tp_gather(buf, first, count, start, size):
+    def o_gather_of(p):
         def at(slot):
-            def region(half):
-                return buf.at[slot, pl.ds(first + half * (count // 2), count // 2), pl.ds(start, size)]
-            return region
+            return lambda half: oall.at[slot, pl.ds(p * piece + half * (piece // 2), piece // 2)]
         return RingGather(copies, up, down, at(0), at(3), at(1), at(2), at(3), at(1), at(2))
 
-    o_gather = [tp_gather(oall, p * piece, piece, 0, head_cols) for p in (0, 1)]
-    y_gather = {(p, n): tp_gather(yall, p * piece, piece, start, size)
-                for p in (0, 1) for n, (start, size) in enumerate(col_chunks)}
+    def y_gather_of(p, n):
+        start, size = col_chunks[n]
+
+        def at(step):
+            cols = pl.ds(pl.multiple_of(tp_at(step) * out_cols + start, 128), size)
+            return lambda half: y_out.at[pl.ds(p * piece + half * (piece // 2), piece // 2), cols]
+
+        def passed(half):
+            return at(3 if half == 0 else 1)(half)
+        return RingGather(copies, up, down, at(0), at(3), at(1), at(2), at(0), at(0), passed)
+
+    o_gather = [o_gather_of(p) for p in (0, 1)]
+    y_gather = {(p, n): y_gather_of(p, n) for p in (0, 1) for n in range(len(col_chunks))}
 
     loads['pos'].wait()
     loads['freq'].wait()
@@ -224,19 +227,23 @@
         pos_row = pos_v[:, pl.ds(p * piece, piece)].astype(F32)
         return jnp.transpose(jnp.broadcast_to(pos_row, (piece, piece)))
 
-    for p in (0, 1):
-        angle = pos_column(p) * freq
-        sine = jnp.sin(angle)
-        cos_v[pl.ds(p * piece, piece), :] = jnp.cos(angle)
-        sin_v[pl.ds(p * piece, piece), :] = jnp.where(lower, -sine, sine)
+    angle = jnp.where(lower, pos_column(0), pos_column(1)) * freq
+    cosine, sine = jnp.cos(angle), jnp.sin(angle)
+    cosine_turned, sine_turned = pltpu.roll(cosine, half_dim, 1), pltpu.roll(sine, half_dim, 1)
+    cos_v[0] = jnp.where(lower, cosine, cosine_turned)
+    cos_v[1] = jnp.where(lower, cosine_turned, cosine)
+    sin_v[0] = jnp.where(lower, -sine, sine_turned)
+    sin_v[1] = jnp.where(lower, -sine_turned, sine)
 
     def rope(vec, p):
         vec = vec.astype(F32)
-        part = pl.ds(p * piece, piece)
-        return (vec * cos_v[part, :] + pltpu.roll(vec, half_dim, 1) * sin_v[part, :]).astype(BF16)
+        return (vec * cos_v[p] + pltpu.roll(vec, half_dim, 1) * sin_v[p]).astype(BF16)
 
     loads['gain'].wait()
-    norm_rows = 16
+    for tile in range(width // 128):
+        gain_v[:, tile * 128:(tile + 1) * 128] = gain_raw[tile:tile + 1, :]
+
+    norm_rows = 32
     for p in (0, 1):
         loads['x', p].wait()
 
@@ -247,24 +254,24 @@
             hv[part, :] = (x_f32 * inv_rms * gain_v[...]).astype(BF16)
             return 0
         lax.fori_loop(0, piece // norm_rows, norm_step, 0)
-
-    loads['wk'].wait()
-    loads['wv'].wait()
-    kv_new = jnp.dot(hv[...], wkv[...], preferred_element_type=F32).astype(BF16)
-    for p in (0, 1):
-        block = kv_new[p * piece:(p + 1) * piece]
-        kv_region(p)(c, 0)[...] = rope(block[:, :head_dim], p)
-        kv_region(p)(c, 1)[...] = block[:, head_dim:]
+        if p == 0:
+            loads['wk'].wait()
+            loads['wv'].wait()
+            for first, count in q_chunks:
+                cols = pl.ds(first * head_dim, count * head_dim)
+                load(('wq', first), wq_hbm.at[:, cols], wq.at[:, cols])
+            pl.semaphore_wait(barrier, len(peers))
+        block = jnp.dot(hv[pl.ds(p * piece, piece), :], wkv[...], preferred_element_type=F32).astype(BF16)
+        k_new, v_new = rope(block[:, :head_dim], p), block[:, head_dim:]
+        kv_region(p)(c, 0)[...] = k_new
+        kv_region(p)(c, 1)[...] = v_new
         kv_gather[p].send()
-    stores = []
-
-    def store(src, dst):
-        stores.append(pltpu.make_async_copy(src, dst, store_sem.at[len(stores)]))
-        stores[-1].start()
-
-    for p in (0, 1):
-        store(kv_region(p)(c, 0), kc_hbm.at[pl.ds(p * piece, piece)])
-        store(kv_region(p)(c, 1), vc_hbm.at[pl.ds(p * piece, piece)])
+        kc_out[pl.ds(p * piece, piece), :] = k_new
+        vc_out[pl.ds(p * piece, piece), :] = v_new
+        if p == 0:
+            for copy in wo_out.values():
+                copy.start()
+    load('wo', wo_hbm.at[:, pl.ds(own_cols, out_cols)], wo.at[0])
 
     def queries(first, count):
         loads['wq', first].wait()
@@ -274,86 +281,94 @@
                 qs[p, pl.ds((first + h) * piece, piece), :] = rope(
                     new[p * piece:(p + 1) * piece, h * head_dim:(h + 1) * head_dim], p)
 
-    queries(*q_chunks[0])
-    for p in (0, 1):
-        kv_gather[p].relay()
-    queries(*q_chunks[1])
-    for p in (0, 1):
-        kv_gather[p].near()
-    for p in (0, 1):
-        kv_gather[p].last()
-
-    def attend(p):
-        low_blocks = (chip + 1) if p == 0 else chips
-        blocks = low_blocks if p == 0 else low_blocks + chips - chip
+    def key_rows(block):
+        return pl.ds(pl.multiple_of(block * KEY_BLOCK, KEY_BLOCK), KEY_BLOCK)
+
+    def open_piece(p):
+        run_max[...] = jnp.full(run_max.shape, LOWEST, F32)
+        run_sum[...] = jnp.zeros(run_sum.shape, F32)
+        acc[...] = jnp.zeros(acc.shape, F32)
+
+    def score_blocks(p, count, block_of, slot_of):
         piece_id = c if p == 0 else 2 * cp_size - 1 - c
-        pos_col = pos_column(p)
         q_idx = (piece_id * piece).astype(F32) + lax.broadcasted_iota(jnp.int32, (piece, piece), 0).astype(F32)
-        doc_start = q_idx - pos_col
+        doc_start = q_idx - pos_column(p)
         lane = lax.broadcasted_iota(jnp.int32, (piece, piece), 1).astype(F32)
-        run_max[...] = jnp.full(run_max.shape, -jnp.inf, F32)
-        run_sum[...] = jnp.zeros(run_sum.shape, F32)
-
-        def key_rows(step):
-            block = jnp.where(step < low_blocks, step, step - low_blocks + chip + chips)
-            return block, pl.ds(pl.multiple_of(block * KEY_BLOCK, KEY_BLOCK), KEY_BLOCK)
 
         def score_step(step, _):
-            block, part = key_rows(step)
+            block, slot = block_of(step), slot_of(step)
             for half in (0, 1):
                 owner = block * 2 + half
                 owner_piece = jnp.where(owner < cp_size, owner, 3 * cp_size - 1 - owner)
                 key_idx = (owner_piece * piece).astype(F32) + lane
                 seen = (key_idx >= doc_start) & (key_idx <= q_idx)
                 cap_v[:, half * piece:(half + 1) * piece] = jnp.where(seen, jnp.inf, -jnp.inf)
-            raw = lax.dot_general(qs[p], kv[0, part, :], (((1,), (1,)), ((), ())), preferred_element_type=F32)
+            raw = lax.dot_general(qs[p], kv[0, key_rows(block), :], (((1,), (1,)), ((), ())),
+                                  preferred_element_type=F32)
             for h in range(heads):
                 mine = slice(h * piece, (h + 1) * piece)
-                capped = jnp.minimum(raw[mine], cap_v[...])
-                scores[step, mine, :] = capped
-                run_max[mine, :] = jnp.maximum(run_max[mine, :], jnp.maximum(capped[:, :piece], capped[:, piece:]))
+                capped = jnp.minimum(raw[mine] * score_scale, cap_v[...])
+                scores[slot, mine, :] = capped
+                one, two = capped[:, :piece], capped[:, piece:]
+                before = run_max[mine, :]
+                top = jnp.maximum(before, jnp.maximum(one, two))
+                run_max[mine, :] = top
+                run_sum[mine, :] = (run_sum[mine, :] * jnp.exp2(before - top)
+                                    + (jnp.exp2(one - top) + jnp.exp2(two - top)))
             return 0
-        lax.fori_loop(0, blocks, score_step, 0)
+        lax.fori_loop(0, count, score_step, 0)
+
+    def close_scores():
         for h in range(heads):
             mine = slice(h * piece, (h + 1) * piece)
-            top = jnp.max(run_max[mine, :], axis=-1, keepdims=True) * score_scale
-            run_max[mine, :] = jnp.broadcast_to(top, (piece, piece))
-
-        def sum_step(step, _):
-            for h in range(heads):
-                mine = slice(h * piece, (h + 1) * piece)
-                shift = run_max[mine, :]
-                run_sum[mine, :] += (jnp.exp2(scores[step, mine, :piece] * score_scale - shift)
-                                     + jnp.exp2(scores[step, mine, piece:] * score_scale - shift))
+            lane_max = run_max[mine, :]
+            top = jnp.broadcast_to(jnp.max(lane_max, axis=-1, keepdims=True), (piece, piece))
+            total = jnp.sum(run_sum[mine, :] * jnp.exp2(lane_max - top), axis=-1, keepdims=True)
+            run_max[mine, :] = top + jnp.broadcast_to(jnp.log2(total), (piece, piece))
+
+    def value_blocks(count, block_of, slot_of):
+        def value_step(step, _):
+            block, slot = block_of(step), slot_of(step)
+            shift = run_max[...]
+            probs = jnp.concatenate([jnp.exp2(scores[slot, :, :piece] - shift).astype(BF16),
+                                     jnp.exp2(scores[slot, :, piece:] - shift).astype(BF16)], axis=-1)
+            acc[...] += jnp.dot(probs, kv[1, key_rows(block), :], preferred_element_type=F32)
             return 0
-        lax.fori_loop(0, blocks, sum_step, 0)
-        for h in range(heads):
-            mine = slice(h * piece, (h + 1) * piece)
-            total = jnp.sum(run_sum[mine, :], axis=-1, keepdims=True)
-            run_max[mine, :] = run_max[mine, :] + jnp.broadcast_to(jnp.log2(total), (piece, piece))
-        acc[...] = jnp.zeros(acc.shape, F32)
-
-        def value_step(step, _):
-            _, part = key_rows(step)
-            shift = run_max[...]
-            probs = jnp.concatenate([jnp.exp2(scores[step, :, :piece] * score_scale - shift).astype(BF16),
-                                     jnp.exp2(scores[step, :, piece:] * score_scale - shift).astype(BF16)], axis=-1)
-            acc[...] += jnp.dot(probs, kv[1, part, :], preferred_element_type=F32)
-            return 0
-        lax.fori_loop(0, blocks, value_step, 0)
+        lax.fori_loop(0, count, value_step, 0)
+
+    def close_piece(p):
         for h in range(heads):
             oall[0, pl.ds(p * piece, piece), h * head_dim:(h + 1) * head_dim] = (
                 acc[h * piece:(h + 1) * piece, :].astype(BF16))
-
+        o_gather[p].send()
+
+    def same(step):
+        return step
+
+    queries(*q_chunks[0])
+    kv_gather[0].relay()
+    queries(*q_chunks[1])
+    kv_gather[1].relay()
+    kv_gather[0].near()
+    kv_gather[0].last()
+    kv_gather[1].near()
     for step in range(1, tp_size):
         wo_in[0, step].wait_recv()
     wo_gather[0].send()
     kv_gather[0].finish()
+    open_piece(0)
+    score_blocks(0, chip + 1, same, same)
+    close_scores()
+    value_blocks(chip + 1, same, same)
+    close_piece(0)
+    kv_gather[1].last()
+    open_piece(1)
+    score_blocks(1, chips, same, same)
     kv_gather[1].finish()
-    attend(0)
-    o_gather[0].send()
-    attend(1)
-    o_gather[1].send()
+    score_blocks(1, chips - chip, lambda step: step + chips + chip, lambda step: step + chips)
+    close_scores()
+    value_blocks(2 * chips - chip, lambda step: jnp.where(step < chips, step, step + chip), same)
+    close_piece(1)
 
     wo_gather[0].relay()
     o_gather[0].relay()
@@ -375,15 +390,8 @@
         mixed = jnp.dot(oall[0, part, :], wo[0, :, pl.ds(start, size)], preferred_element_type=F32)
         for slot in range(1, tp_size):
             mixed = mixed + jnp.dot(oall[slot, part, :], wo[slot, :, pl.ds(start, size)], preferred_element_type=F32)
-        yall[0, part, pl.ds(start, size)] = (total + mixed).astype(BF16)
+        y_out[part, pl.ds(pl.multiple_of(own_cols + start, 128), size)] = (total + mixed).astype(BF16)
         y_gather[p, n].send()
-
-    def put(p, n):
-        start, size = col_chunks[n]
-        part = pl.ds(p * piece, piece)
-        for slot in range(tp_size):
-            store(yall.at[slot, part, pl.ds(start, size)],
-                  y_hbm.at[part, pl.ds(pl.multiple_of(tp_at(slot) * out_cols + start, 128), size)])
 
     project(0, 0)
     o_gather[1].near()
@@ -399,25 +407,19 @@
     project(1, 1)
     y_gather[0, 0].near()
     y_gather[0, 0].last()
-    put(0, 0)
     y_gather[0, 1].relay()
     y_gather[1, 0].near()
     y_gather[1, 0].last()
-    put(1, 0)
     y_gather[1, 1].relay()
     y_gather[0, 1].near()
     y_gather[0, 1].last()
-    put(0, 1)
     y_gather[1, 1].near()
     y_gather[1, 1].last()
-    put(1, 1)
 
     for copy in wo_out.values():
         copy.wait_send()
     for gather in kv_gather + wo_gather + o_gather + list(y_gather.values()):
         gather.drain()
-    for copy in stores:
-        copy.wait()
     assert copies.used == send_sem.shape[0]
 
 
@@ -438,11 +440,12 @@
             lambda *refs: layer_kernel(tp_size, cp_size, *refs),
             out_shape=(jax.ShapeDtypeStruct(x_in.shape, BF16), jax.ShapeDtypeStruct((rows, head_dim), BF16),
                        jax.ShapeDtypeStruct((rows, head_dim), BF16)),
-            in_specs=[pl.BlockSpec(memory_space=pl.ANY)] * 8,
-            out_specs=[pl.BlockSpec(memory_space=pl.ANY)] * 3,
+            in_specs=[pl.BlockSpec(memory_space=pltpu.HBM)] * 8,
+            out_specs=[pl.BlockSpec(memory_space=pltpu.VMEM)] * 3,
             scratch_shapes=[
                 pltpu.VMEM((rows, width), BF16),
                 pltpu.VMEM((rows, width), BF16),
+                pltpu.VMEM((width // 128, 128), F32),
                 pltpu.VMEM((1, width), F32),
                 pltpu.VMEM((1, rows), jnp.int32),
                 pltpu.VMEM((1, head_dim // 2), F32),
@@ -451,25 +454,24 @@
                 pltpu.VMEM((tp_size, head_cols, out_cols), BF16),
                 pltpu.VMEM((2, rows * cp_size, head_dim), BF16),
                 pltpu.VMEM((2, stack, head_dim), BF16),
-                pltpu.VMEM((rows, head_dim), F32),
-                pltpu.VMEM((rows, head_dim), F32),
+                pltpu.VMEM((2, piece, head_dim), F32),
+                pltpu.VMEM((2, piece, head_dim), F32),
                 pltpu.VMEM((piece, KEY_BLOCK), F32),
                 pltpu.VMEM((rows * cp_size // KEY_BLOCK, stack, KEY_BLOCK), F32),
                 pltpu.VMEM((stack, piece), F32),
                 pltpu.VMEM((stack, piece), F32),
                 pltpu.VMEM((stack, head_dim), F32),
                 pltpu.VMEM((tp_size, rows, head_cols), BF16),
-                pltpu.VMEM((tp_size, rows, out_cols), BF16),
                 pltpu.SemaphoreType.DMA((10,)),
-                pltpu.SemaphoreType.DMA((4 + 4 * tp_size,)),
                 pltpu.SemaphoreType.DMA((copies,)),
                 pltpu.SemaphoreType.DMA((copies,)),
             ],
             compiler_params=pltpu.CompilerParams(
-                collective_id=0, has_side_effects=True, vmem_limit_bytes=60 * 1024 * 1024),
+                collective_id=0, has_side_effects=True, vmem_limit_bytes=44 * 1024 * 1024),
             name='layer',
-        )(x_in, pos_in_doc.reshape(1, rows), norm_gain.reshape(1, width), w_q, w_k, w_v, w_o,
-          inv_freq.reshape(1, head_dim // 2))
+        )(*[pltpu.with_memory_space_constraint(a, pltpu.HBM) for a in (
+            x_in, pos_in_doc.reshape(1, rows), norm_gain.reshape(width // 128, 128), w_q, w_k, w_v, w_o,
+            inv_freq.reshape(1, head_dim // 2))])
         kv_heads = 1
         return y_out, k_new.reshape(rows, kv_heads, head_dim), v_new.reshape(rows, kv_heads, head_dim)
 

time: 66 us -> 57.4 us (0.87)
  Pallas kernels: 59.6 us -> 54.2 us
  local copies, waits for them, and re-layouts: 5.48 us -> 2.49 us
    pallas_call x1, Pallas kernels: 59.6 us -> 54.2 us  [local_step(): pl.pallas_call(lambda *refs: layer_kernel(tp_size, cp_size, *refs), out_s...]
    unnamed x7 -> x3, local copies, waits for them, and re-layouts: 4.15 us -> 2.49 us
    reshape x1 -> x0, local copies, waits for them, and re-layouts: 1.33 us -> none  [local_step(): norm_gain.reshape(1, width)]
where the time goes in v2:
time: 57.4 us; the launch traced here: 57.3 us
  Pallas kernels  54.2 us (94%)
  local copies, waits for them, and re-layouts  2.49 us (4%)
  between operations  0.64 us (1%)
    pallas_call x1, Pallas kernels, local_step(): pl.pallas_call(lambda *refs: layer_kernel(tp_size, cp_size, *refs), out_s...  54.2 us
    unnamed x3, local copies, waits for them, and re-layouts  2.49 us

profile of v2, /device:TPU:97, one launch (start us, length us, event | category | flops | bytes accessed | tf_op | source)
XLA Modules:
  0.0 57.3 jit_solution(14166825465329295558)
XLA Ops:
  0.6 54.2 %layer.1 = (bf16[256,3584]{1,0:T(8,128)(2,1)S(1)}, bf16[256,128]{1,0:T(8,128)(2,1)S(1)}, bf16[256,128]{1,0:T(8,128)(2,1)S(1)}) custom-call(bf16[256,3584]{1,0:T(8,128)(2,1)} %refs_0_.1, s32[1,256]{1,0:T(1,128)} %bitcast.8, f32[28,128]{1,0:T(8,128)} %bitcast.7, bf16[3584,896]{1,0:T(8,128)(2,1)} %refs_3_.1, bf16[3584,128]{1,0:T(8,128)(2,1)} %refs_4_.1, ...), custom_call_target="tpu_custom_call" | custom-call | tf_op jit(solution)/shard_map/layer/pallas_call | solution.py:439
  54.8 1.2 %copy.14 = bf16[256,3584]{1,0:T(8,128)(2,1)} copy(bf16[256,3584]{1,0:T(8,128)(2,1)S(1)} %get-tuple-element.12) | data formatting | bytes 3670016
  56.1 0.6 %copy.15 = bf16[256,1,128]{2,0,1:T(8,128)(2,1)} copy(bf16[256,1,128]{2,0,1:T(8,128)(2,1)S(1)} %bitcast.6) | data formatting | bytes 131072
  56.7 0.6 %copy.16 = bf16[256,1,128]{2,0,1:T(8,128)(2,1)} copy(bf16[256,1,128]{2,0,1:T(8,128)(2,1)S(1)} %bitcast.5) | data formatting | bytes 131072

commit v3 on v2

--- a/solution.py
+++ b/solution.py
@@ -107,6 +107,41 @@
     def drain(self):
         self.ring.drain()
         for copy in self.out.values():
+            copy.wait_send()
+
+
+class DirectGather:
+    def __init__(self, copies, right_dev, left_dev, far_dev, sib_dev, region, own, left, right, far, other):
+        self.out, self.got, self.hand, self.back = [], {}, {}, {}
+        for name, dev, owner in (('left', right_dev, left), ('right', left_dev, right), ('far', far_dev, far)):
+            index = copies.take(1)
+            self.out.append(copies.make(index, region(own), region(own), dev))
+            self.got[name] = copies.make(index, region(owner), region(owner), dev)
+        for name, owner in (('own', own), ('left', left), ('right', right), ('far', far)):
+            index = copies.take(1)
+            self.hand[name] = copies.make(index, region(owner), region(owner), sib_dev)
+            self.back[name] = copies.make(index, region(other(owner)), region(other(owner)), sib_dev)
+
+    def send(self):
+        for copy in self.out:
+            copy.start()
+        self.hand['own'].start()
+
+    def near(self):
+        for name in ('left', 'right'):
+            self.got[name].wait_recv()
+            self.hand[name].start()
+
+    def last(self):
+        self.got['far'].wait_recv()
+        self.hand['far'].start()
+
+    def finish(self):
+        for name in ('left', 'right', 'far'):
+            self.back[name].wait_recv()
+
+    def drain(self):
+        for copy in self.out + list(self.hand.values()):
             copy.wait_send()
 
 
@@ -142,7 +177,7 @@
         return owner + 1 - 2 * core
 
     up, down = {'tp': tp_at(1)}, {'tp': tp_at(tp_size - 1)}
-    right, left, sib = {'cp': cp_at(1)}, {'cp': cp_at(chips - 1)}, {'cp': other(c)}
+    right, left, far, sib = {'cp': cp_at(1)}, {'cp': cp_at(chips - 1)}, {'cp': cp_at(2)}, {'cp': other(c)}
 
     loads = {}
 
@@ -161,13 +196,13 @@
     q_chunks = ((0, 4), (4, heads - 4))
 
     barrier = pltpu.get_barrier_semaphore()
-    peers = [{'tp': tp_at(step)} for step in range(1, tp_size)] + [right, left, sib]
+    peers = [{'tp': tp_at(step)} for step in range(1, tp_size)] + [right, left, far, sib]
     for peer in peers:
         pl.semaphore_signal(barrier, inc=1, device_id=peer, device_id_type=MESH)
 
     copies = Copies(send_sem, recv_sem)
 
-    col_chunks = ((0, 512), (512, out_cols - 512))
+    col_chunks = ((0, 384), (384, 256), (640, out_cols - 640))
     share_row = pl.multiple_of(c * share, 16)
     wo_out, wo_in = {}, {}
     for n, (start, size) in enumerate(col_chunks):
@@ -188,15 +223,16 @@
             return wo.at[pl.ds(1, tp_size - 1), pl.ds(first, share - cut if half else cut), pl.ds(start, size)]
         return region
 
-    def kv_region(p):
-        def region(owner, half):
-            return kv.at[half, pl.ds(pl.multiple_of(p * low_rows + owner * piece, piece), piece)]
+    def kv_region(p, kind):
+        def region(owner):
+            return kv.at[kind, pl.ds(pl.multiple_of(p * low_rows + owner * piece, piece), piece)]
         return region
 
     def chip_gather(region):
         return ChipGather(copies, right, left, sib, region, c, cp_at(chips - 1), cp_at(1), cp_at(2), other)
 
-    kv_gather = [chip_gather(kv_region(p)) for p in (0, 1)]
+    kv_gather = {(p, kind): DirectGather(copies, right, left, far, sib, kv_region(p, kind), c, cp_at(chips - 1), cp_at(1),
+                                         cp_at(2), other) for p in (0, 1) for kind in (0, 1)}
     wo_gather = [chip_gather(wo_region(n)) for n in range(len(col_chunks))]
 
     def o_gather_of(p):
@@ -261,16 +297,16 @@
                 cols = pl.ds(first * head_dim, count * head_dim)
                 load(('wq', first), wq_hbm.at[:, cols], wq.at[:, cols])
             pl.semaphore_wait(barrier, len(peers))
+            for copy in wo_out.values():
+                copy.start()
         block = jnp.dot(hv[pl.ds(p * piece, piece), :], wkv[...], preferred_element_type=F32).astype(BF16)
         k_new, v_new = rope(block[:, :head_dim], p), block[:, head_dim:]
-        kv_region(p)(c, 0)[...] = k_new
-        kv_region(p)(c, 1)[...] = v_new
-        kv_gather[p].send()
+        kv_region(p, 0)(c)[...] = k_new
+        kv_gather[p, 0].send()
+        kv_region(p, 1)(c)[...] = v_new
+        kv_gather[p, 1].send()
         kc_out[pl.ds(p * piece, piece), :] = k_new
         vc_out[pl.ds(p * piece, piece), :] = v_new
-        if p == 0:
-            for copy in wo_out.values():
-                copy.start()
     load('wo', wo_hbm.at[:, pl.ds(own_cols, out_cols)], wo.at[0])
 
     def queries(first, count):
@@ -284,104 +320,71 @@
     def key_rows(block):
         return pl.ds(pl.multiple_of(block * KEY_BLOCK, KEY_BLOCK), KEY_BLOCK)
 
-    def open_piece(p):
-        run_max[...] = jnp.full(run_max.shape, LOWEST, F32)
-        run_sum[...] = jnp.zeros(run_sum.shape, F32)
-        acc[...] = jnp.zeros(acc.shape, F32)
-
-    def score_blocks(p, count, block_of, slot_of):
+    run_max[...] = jnp.full(run_max.shape, LOWEST, F32)
+    run_sum[...] = jnp.zeros(run_sum.shape, F32)
+
+    def score(p, blocks):
         piece_id = c if p == 0 else 2 * cp_size - 1 - c
         q_idx = (piece_id * piece).astype(F32) + lax.broadcasted_iota(jnp.int32, (piece, piece), 0).astype(F32)
         doc_start = q_idx - pos_column(p)
         lane = lax.broadcasted_iota(jnp.int32, (piece, piece), 1).astype(F32)
-
-        def score_step(step, _):
-            block, slot = block_of(step), slot_of(step)
+        for n, block in enumerate(blocks):
             for half in (0, 1):
                 owner = block * 2 + half
                 owner_piece = jnp.where(owner < cp_size, owner, 3 * cp_size - 1 - owner)
                 key_idx = (owner_piece * piece).astype(F32) + lane
                 seen = (key_idx >= doc_start) & (key_idx <= q_idx)
-                cap_v[:, half * piece:(half + 1) * piece] = jnp.where(seen, jnp.inf, -jnp.inf)
-            raw = lax.dot_general(qs[p], kv[0, key_rows(block), :], (((1,), (1,)), ((), ())),
-                                  preferred_element_type=F32)
-            for h in range(heads):
-                mine = slice(h * piece, (h + 1) * piece)
-                capped = jnp.minimum(raw[mine] * score_scale, cap_v[...])
-                scores[slot, mine, :] = capped
-                one, two = capped[:, :piece], capped[:, piece:]
-                before = run_max[mine, :]
-                top = jnp.maximum(before, jnp.maximum(one, two))
-                run_max[mine, :] = top
-                run_sum[mine, :] = (run_sum[mine, :] * jnp.exp2(before - top)
-                                    + (jnp.exp2(one - top) + jnp.exp2(two - top)))
-            return 0
-        lax.fori_loop(0, count, score_step, 0)
-
-    def close_scores():
+                cap_v[n, :, half * piece:(half + 1) * piece] = jnp.where(seen, jnp.inf, -jnp.inf)
+        raw = [lax.dot_general(qs[p], kv[0, key_rows(block), :], (((1,), (1,)), ((), ())), preferred_element_type=F32)
+               for block in blocks]
         for h in range(heads):
             mine = slice(h * piece, (h + 1) * piece)
-            lane_max = run_max[mine, :]
+            parts = []
+            for n, block in enumerate(blocks):
+                capped = jnp.minimum(raw[n][mine] * score_scale, cap_v[n])
+                scores[block + p * chips, mine, :] = capped
+                parts += [capped[:, :piece], capped[:, piece:]]
+            before = run_max[p, mine, :]
+            top = before
+            for part in parts:
+                top = jnp.maximum(top, part)
+            run_max[p, mine, :] = top
+            total = run_sum[p, mine, :] * jnp.exp2(before - top)
+            for part in parts:
+                total = total + jnp.exp2(part - top)
+            run_sum[p, mine, :] = total
+
+    def score_loop(p, count, block_of):
+        def step(i, _):
+            score(p, [block_of(i)])
+            return 0
+        lax.fori_loop(0, count, step, 0)
+
+    def close_scores(p):
+        for h in range(heads):
+            mine = slice(h * piece, (h + 1) * piece)
+            lane_max = run_max[p, mine, :]
             top = jnp.broadcast_to(jnp.max(lane_max, axis=-1, keepdims=True), (piece, piece))
-            total = jnp.sum(run_sum[mine, :] * jnp.exp2(lane_max - top), axis=-1, keepdims=True)
-            run_max[mine, :] = top + jnp.broadcast_to(jnp.log2(total), (piece, piece))
-
-    def value_blocks(count, block_of, slot_of):
-        def value_step(step, _):
-            block, slot = block_of(step), slot_of(step)
-            shift = run_max[...]
-            probs = jnp.concatenate([jnp.exp2(scores[slot, :, :piece] - shift).astype(BF16),
-                                     jnp.exp2(scores[slot, :, piece:] - shift).astype(BF16)], axis=-1)
+            total = jnp.sum(run_sum[p, mine, :] * jnp.exp2(lane_max - top), axis=-1, keepdims=True)
+            run_max[p, mine, :] = top + jnp.broadcast_to(jnp.log2(total), (piece, piece))
+
+    def value_loop(p, count, block_of):
+        acc[...] = jnp.zeros(acc.shape, F32)
+
+        def step(i, _):
+            block = block_of(i)
+            shift = run_max[p]
+            probs = jnp.concatenate([jnp.exp2(scores[block + p * chips, :, :piece] - shift).astype(BF16),
+                                     jnp.exp2(scores[block + p * chips, :, piece:] - shift).astype(BF16)], axis=-1)
             acc[...] += jnp.dot(probs, kv[1, key_rows(block), :], preferred_element_type=F32)
             return 0
-        lax.fori_loop(0, count, value_step, 0)
+        lax.fori_loop(0, count, step, 0)
 
     def close_piece(p):
         for h in range(heads):
             oall[0, pl.ds(p * piece, piece), h * head_dim:(h + 1) * head_dim] = (
                 acc[h * piece:(h + 1) * piece, :].astype(BF16))
         o_gather[p].send()
-
-    def same(step):
-        return step
-
-    queries(*q_chunks[0])
-    kv_gather[0].relay()
-    queries(*q_chunks[1])
-    kv_gather[1].relay()
-    kv_gather[0].near()
-    kv_gather[0].last()
-    kv_gather[1].near()
-    for step in range(1, tp_size):
-        wo_in[0, step].wait_recv()
-    wo_gather[0].send()
-    kv_gather[0].finish()
-    open_piece(0)
-    score_blocks(0, chip + 1, same, same)
-    close_scores()
-    value_blocks(chip + 1, same, same)
-    close_piece(0)
-    kv_gather[1].last()
-    open_piece(1)
-    score_blocks(1, chips, same, same)
-    kv_gather[1].finish()
-    score_blocks(1, chips - chip, lambda step: step + chips + chip, lambda step: step + chips)
-    close_scores()
-    value_blocks(2 * chips - chip, lambda step: jnp.where(step < chips, step, step + chip), same)
-    close_piece(1)
-
-    wo_gather[0].relay()
-    o_gather[0].relay()
-    for step in range(1, tp_size):
-        wo_in[1, step].wait_recv()
-    wo_gather[1].send()
-    wo_gather[0].near()
-    o_gather[0].near()
-    o_gather[1].relay()
-    wo_gather[0].last()
-    o_gather[0].last()
-    loads['wo'].wait()
-    wo_gather[0].finish()
 
     def project(p, n):
         start, size = col_chunks[n]
@@ -391,34 +394,90 @@
         for slot in range(1, tp_size):
             mixed = mixed + jnp.dot(oall[slot, part, :], wo[slot, :, pl.ds(start, size)], preferred_element_type=F32)
         y_out[part, pl.ds(pl.multiple_of(own_cols + start, 128), size)] = (total + mixed).astype(BF16)
-        y_gather[p, n].send()
-
+
+    def wo_send(n):
+        for step in range(1, tp_size):
+            wo_in[n, step].wait_recv()
+        wo_gather[n].send()
+
+    queries(*q_chunks[0])
+    kv_gather[0, 0].near()
+    queries(*q_chunks[1])
+    kv_gather[0, 0].back['own'].wait_recv()
+    score(0, [chip])
+    kv_gather[0, 0].last()
+    kv_gather[0, 1].near()
+    score(1, [chip])
+    kv_gather[1, 0].back['own'].wait_recv()
+    score(1, [chips + chip])
+    wo_send(0)
+    kv_gather[0, 0].finish()
+    score_loop(0, chip, lambda i: i)
+    close_scores(0)
+    kv_gather[0, 1].last()
+    kv_gather[0, 1].back['own'].wait_recv()
+    kv_gather[0, 1].finish()
+    value_loop(0, chip + 1, lambda i: i)
+    close_piece(0)
+    kv_gather[1, 0].near()
+    kv_gather[1, 0].last()
+    score(1, [lax.rem(chip + i, chips) for i in range(1, chips)])
+    wo_gather[0].relay()
+    wo_send(1)
+    kv_gather[1, 1].near()
+    kv_gather[1, 0].finish()
+    score_loop(1, chips - 1 - chip, lambda i: chips + chip + 1 + i)
+    kv_gather[1, 1].last()
+    close_scores(1)
+    o_gather[0].relay()
+    kv_gather[1, 1].back['own'].wait_recv()
+    kv_gather[1, 1].finish()
+    value_loop(1, 2 * chips - chip, lambda i: jnp.where(i < chips, i, i + chip))
+    close_piece(1)
+
+    o_gather[0].near()
+    wo_gather[0].near()
+    wo_gather[0].last()
+    o_gather[0].last()
+    wo_gather[1].relay()
+    wo_send(2)
+    loads['wo'].wait()
+    wo_gather[0].finish()
     project(0, 0)
-    o_gather[1].near()
-    wo_gather[1].relay()
-    o_gather[1].last()
-    project(1, 0)
-    y_gather[0, 0].relay()
+    o_gather[1].relay()
+    y_gather[0, 0].send()
     wo_gather[1].near()
     wo_gather[1].last()
     wo_gather[1].finish()
     project(0, 1)
+    y_gather[0, 1].send()
+    wo_gather[2].relay()
+    o_gather[1].near()
+    o_gather[1].last()
+    project(1, 0)
+    y_gather[1, 0].send()
+    project(1, 1)
+    y_gather[1, 1].send()
+    y_gather[0, 0].relay()
+    wo_gather[2].near()
+    y_gather[0, 1].relay()
+    wo_gather[2].last()
+    wo_gather[2].finish()
+    project(0, 2)
+    y_gather[0, 2].send()
+    project(1, 2)
+    y_gather[1, 2].send()
     y_gather[1, 0].relay()
-    project(1, 1)
-    y_gather[0, 0].near()
-    y_gather[0, 0].last()
-    y_gather[0, 1].relay()
-    y_gather[1, 0].near()
-    y_gather[1, 0].last()
     y_gather[1, 1].relay()
-    y_gather[0, 1].near()
-    y_gather[0, 1].last()
-    y_gather[1, 1].near()
-    y_gather[1, 1].last()
+    y_gather[0, 2].relay()
+    y_gather[1, 2].relay()
+    for gather in y_gather.values():
+        gather.near()
+        gather.last()
 
     for copy in wo_out.values():
         copy.wait_send()
-    for gather in kv_gather + wo_gather + o_gather + list(y_gather.values()):
+    for gather in list(kv_gather.values()) + wo_gather + o_gather + list(y_gather.values()):
         gather.drain()
     assert copies.used == send_sem.shape[0]
 
@@ -434,7 +493,7 @@
         head_cols = w_q.shape[1]
         heads = head_cols // head_dim
         out_cols = width // tp_size
-        copies = 2 * (tp_size - 1) + 4 * 14 + 6 * 6
+        copies = 3 * (tp_size - 1) + 4 * 7 + 3 * 14 + 8 * 6
         stack = heads * piece
         y_out, k_new, v_new = pl.pallas_call(
             lambda *refs: layer_kernel(tp_size, cp_size, *refs),
@@ -456,10 +515,10 @@
                 pltpu.VMEM((2, stack, head_dim), BF16),
                 pltpu.VMEM((2, piece, head_dim), F32),
                 pltpu.VMEM((2, piece, head_dim), F32),
-                pltpu.VMEM((piece, KEY_BLOCK), F32),
-                pltpu.VMEM((rows * cp_size // KEY_BLOCK, stack, KEY_BLOCK), F32),
-                pltpu.VMEM((stack, piece), F32),
-                pltpu.VMEM((stack, piece), F32),
+                pltpu.VMEM((cp_size // 2 - 1, piece, KEY_BLOCK), F32),
+                pltpu.VMEM((3 * cp_size // 2, stack, KEY_BLOCK), F32),
+                pltpu.VMEM((2, stack, piece), F32),
+                pltpu.VMEM((2, stack, piece), F32),
                 pltpu.VMEM((stack, head_dim), F32),
                 pltpu.VMEM((tp_size, rows, head_cols), BF16),
                 pltpu.SemaphoreType.DMA((10,)),

time: 57.4 us -> 55.2 us (0.962)
  Pallas kernels: 54.2 us -> 52 us
    pallas_call x1, Pallas kernels: 54.2 us -> 52 us  [local_step(): pl.pallas_call(lambda *refs: layer_kernel(tp_size, cp_size, *refs), out_s...]
where the time goes in v3:
time: 55.2 us
  Pallas kernels  52 us (94%)
  local copies, waits for them, and re-layouts  2.49 us (5%)
  between operations  0.64 us (1%)
    pallas_call x1, Pallas kernels, local_step(): pl.pallas_call(lambda *refs: layer_kernel(tp_size, cp_size, *refs), out_s...  52 us
    unnamed x3, local copies, waits for them, and re-layouts  2.49 us

profile of v3, /device:TPU:97, one launch (start us, length us, event | category | flops | bytes accessed | tf_op | source)
XLA Modules:
  0.0 55.2 jit_solution(6150741990113892329)
XLA Ops:
  0.6 52.0 %layer.1 = (bf16[256,3584]{1,0:T(8,128)(2,1)S(1)}, bf16[256,128]{1,0:T(8,128)(2,1)S(1)}, bf16[256,128]{1,0:T(8,128)(2,1)S(1)}) custom-call(bf16[256,3584]{1,0:T(8,128)(2,1)} %refs_0_.1, s32[1,256]{1,0:T(1,128)} %bitcast.8, f32[28,128]{1,0:T(8,128)} %bitcast.7, bf16[3584,896]{1,0:T(8,128)(2,1)} %refs_3_.1, bf16[3584,128]{1,0:T(8,128)(2,1)} %refs_4_.1, ...), custom_call_target="tpu_custom_call" | custom-call | tf_op jit(solution)/shard_map/layer/pallas_call | solution.py:498
  52.7 1.2 %copy.14 = bf16[256,3584]{1,0:T(8,128)(2,1)} copy(bf16[256,3584]{1,0:T(8,128)(2,1)S(1)} %get-tuple-element.12) | data formatting | bytes 3670016
  53.9 0.6 %copy.15 = bf16[256,1,128]{2,0,1:T(8,128)(2,1)} copy(bf16[256,1,128]{2,0,1:T(8,128)(2,1)S(1)} %bitcast.6) | data formatting | bytes 131072
  54.5 0.6 %copy.16 = bf16[256,1,128]{2,0,1:T(8,128)(2,1)} copy(bf16[256,1,128]{2,0,1:T(8,128)(2,1)S(1)} %bitcast.5) | data formatting | bytes 131072

commit v4 on v3

--- a/solution.py
+++ b/solution.py
@@ -146,7 +146,7 @@
 
 
 def layer_kernel(tp_size, cp_size, x_hbm, pos_hbm, gain_hbm, wq_hbm, wk_hbm, wv_hbm, wo_hbm, freq_hbm,
-                 y_out, kc_out, vc_out,
+                 y_out, kv_out,
                  xv, hv, gain_raw, gain_v, pos_v, freq_v, wkv, wq, wo, kv, qs, cos_v, sin_v, cap_v, scores, run_max,
                  run_sum, acc, oall, load_sem, send_sem, recv_sem):
     rows, width = xv.shape
@@ -305,8 +305,8 @@
         kv_gather[p, 0].send()
         kv_region(p, 1)(c)[...] = v_new
         kv_gather[p, 1].send()
-        kc_out[pl.ds(p * piece, piece), :] = k_new
-        vc_out[pl.ds(p * piece, piece), :] = v_new
+        kv_out[0, pl.ds(p * piece, piece), :] = k_new
+        kv_out[1, pl.ds(p * piece, piece), :] = v_new
     load('wo', wo_hbm.at[:, pl.ds(own_cols, out_cols)], wo.at[0])
 
     def queries(first, count):
@@ -495,12 +495,11 @@
         out_cols = width // tp_size
         copies = 3 * (tp_size - 1) + 4 * 7 + 3 * 14 + 8 * 6
         stack = heads * piece
-        y_out, k_new, v_new = pl.pallas_call(
+        y_out, kv_new = pl.pallas_call(
             lambda *refs: layer_kernel(tp_size, cp_size, *refs),
-            out_shape=(jax.ShapeDtypeStruct(x_in.shape, BF16), jax.ShapeDtypeStruct((rows, head_dim), BF16),
-                       jax.ShapeDtypeStruct((rows, head_dim), BF16)),
+            out_shape=(jax.ShapeDtypeStruct(x_in.shape, BF16), jax.ShapeDtypeStruct((2, rows, head_dim), BF16)),
             in_specs=[pl.BlockSpec(memory_space=pltpu.HBM)] * 8,
-            out_specs=[pl.BlockSpec(memory_space=pltpu.VMEM)] * 3,
+            out_specs=[pl.BlockSpec(memory_space=pltpu.VMEM)] * 2,
             scratch_shapes=[
                 pltpu.VMEM((rows, width), BF16),
                 pltpu.VMEM((rows, width), BF16),
@@ -532,7 +531,7 @@
             x_in, pos_in_doc.reshape(1, rows), norm_gain.reshape(width // 128, 128), w_q, w_k, w_v, w_o,
             inv_freq.reshape(1, head_dim // 2))])
         kv_heads = 1
-        return y_out, k_new.reshape(rows, kv_heads, head_dim), v_new.reshape(rows, kv_heads, head_dim)
+        return y_out, kv_new[0].reshape(rows, kv_heads, head_dim), kv_new[1].reshape(rows, kv_heads, head_dim)
 
     row_spec = P(('dp', 'cp'))
     in_specs = (P(('dp', 'cp'), None), row_spec, row_spec, P(), P(None, 'tp'), P(None, 'tp'), P(None, 'tp'), P('tp', None), P())

time: 55.2 us -> 54.7 us (level)
  local copies, waits for them, and re-layouts: 2.49 us -> 1.89 us
    unnamed x3 -> x1, local copies, waits for them, and re-layouts: 2.49 us -> 1.23 us
    another operation x0 -> x1, local copies, waits for them, and re-layouts: none -> 0.66 us  [local_step(): kv_new[1].reshape(rows, kv_heads, head_dim)]
where the time goes in v4:
time: 54.7 us; the launch traced here: 54.6 us
  Pallas kernels  52.1 us (95%)
  local copies, waits for them, and re-layouts  1.89 us (3%)
  between operations  0.64 us (1%)
    pallas_call x1, Pallas kernels, local_step(): pl.pallas_call(lambda *refs: layer_kernel(tp_size, cp_size, *refs), out_s...  52.1 us
    unnamed x1, local copies, waits for them, and re-layouts  1.23 us

profile of v4, /device:TPU:97, one launch (start us, length us, event | category | flops | bytes accessed | tf_op | source)
XLA Modules:
  0.0 54.6 jit_solution(13536511909837732386)
XLA Ops:
  0.6 52.1 %layer.1 = (bf16[256,3584]{1,0:T(8,128)(2,1)S(1)}, bf16[2,256,128]{2,1,0:T(8,128)(2,1)S(1)}) custom-call(bf16[256,3584]{1,0:T(8,128)(2,1)} %refs_0_.1, s32[1,256]{1,0:T(1,128)} %bitcast.8, f32[28,128]{1,0:T(8,128)} %bitcast.7, bf16[3584,896]{1,0:T(8,128)(2,1)} %refs_3_.1, bf16[3584,128]{1,0:T(8,128)(2,1)} %refs_4_.1, bf16[3584,128]{1,0:T(8,128)(2,1)} %refs_5_.1, ...), custom_call_target="tpu_custom_call" | custom-call | tf_op jit(solution)/shard_map/layer/pallas_call | solution.py:498
  52.7 0.7 %slice_bitcast_fusion = (bf16[256,1,128]{2,0,1:T(8,128)(2,1)}, bf16[256,1,128]{2,0,1:T(8,128)(2,1)}) fusion(bf16[2,256,128]{2,1,0:T(8,128)(2,1)S(1)} %get-tuple-element.6), kind=kLoop, calls=%fused_computation | loop fusion | bytes 262144 | tf_op jit(solution)/shard_map/reshape;squeeze | solution.py:534
  53.4 1.2 %copy.12 = bf16[256,3584]{1,0:T(8,128)(2,1)} copy(bf16[256,3584]{1,0:T(8,128)(2,1)S(1)} %get-tuple-element.12) | data formatting | bytes 3670016

commit v5 on v4

--- a/solution.py
+++ b/solution.py
@@ -110,39 +110,52 @@
             copy.wait_send()
 
 
+def do_if(needed, action):
+    if needed is None:
+        action()
+    else:
+        pl.when(needed)(action)
+
+
 class DirectGather:
-    def __init__(self, copies, right_dev, left_dev, far_dev, sib_dev, region, own, left, right, far, other):
-        self.out, self.got, self.hand, self.back = [], {}, {}, {}
-        for name, dev, owner in (('left', right_dev, left), ('right', left_dev, right), ('far', far_dev, far)):
+    def __init__(self, copies, devs, sib_dev, region, owners, other, gives, takes):
+        self.out, self.got, self.hand, self.back, self.gives, self.takes = {}, {}, {}, {}, gives, takes
+        for name in ('left', 'right', 'far'):
             index = copies.take(1)
-            self.out.append(copies.make(index, region(own), region(own), dev))
-            self.got[name] = copies.make(index, region(owner), region(owner), dev)
-        for name, owner in (('own', own), ('left', left), ('right', right), ('far', far)):
+            self.out[name] = copies.make(index, region(owners['own']), region(owners['own']), devs[name])
+            self.got[name] = copies.make(index, region(owners[name]), region(owners[name]), devs[name])
+        for name, owner in owners.items():
             index = copies.take(1)
             self.hand[name] = copies.make(index, region(owner), region(owner), sib_dev)
             self.back[name] = copies.make(index, region(other(owner)), region(other(owner)), sib_dev)
 
     def send(self):
-        for copy in self.out:
-            copy.start()
+        for name, copy in self.out.items():
+            do_if(self.gives[name], copy.start)
         self.hand['own'].start()
 
-    def near(self):
-        for name in ('left', 'right'):
+    def pass_on(self, name):
+        def action():
             self.got[name].wait_recv()
             self.hand[name].start()
+        do_if(self.takes[name], action)
+
+    def near(self):
+        self.pass_on('left')
+        self.pass_on('right')
 
     def last(self):
-        self.got['far'].wait_recv()
-        self.hand['far'].start()
+        self.pass_on('far')
 
     def finish(self):
         for name in ('left', 'right', 'far'):
-            self.back[name].wait_recv()
+            do_if(self.takes[name], self.back[name].wait_recv)
 
     def drain(self):
-        for copy in self.out + list(self.hand.values()):
-            copy.wait_send()
+        for name, copy in self.out.items():
+            do_if(self.gives[name], copy.wait_send)
+        for name, copy in self.hand.items():
+            do_if(self.takes.get(name), copy.wait_send)
 
 
 def layer_kernel(tp_size, cp_size, x_hbm, pos_hbm, gain_hbm, wq_hbm, wk_hbm, wv_hbm, wo_hbm, freq_hbm,
@@ -231,8 +244,15 @@
     def chip_gather(region):
         return ChipGather(copies, right, left, sib, region, c, cp_at(chips - 1), cp_at(1), cp_at(2), other)
 
-    kv_gather = {(p, kind): DirectGather(copies, right, left, far, sib, kv_region(p, kind), c, cp_at(chips - 1), cp_at(1),
-                                         cp_at(2), other) for p in (0, 1) for kind in (0, 1)}
+    cp_devs = {'left': right, 'right': left, 'far': far}
+    steps = {'left': chips - 1, 'right': 1, 'far': 2}
+    owners = {'own': c, **{name: cp_at(step) for name, step in steps.items()}}
+    always = dict.fromkeys(steps)
+    gives = {name: lax.rem(chip + chips - step, chips) < chip for name, step in steps.items()}
+    takes = {name: lax.rem(chip + step, chips) > chip for name, step in steps.items()}
+    kv_gather = {(p, kind): DirectGather(copies, cp_devs, sib, kv_region(p, kind), owners, other,
+                                         gives if p else always, takes if p else always)
+                 for p in (0, 1) for kind in (0, 1)}
     wo_gather = [chip_gather(wo_region(n)) for n in range(len(col_chunks))]
 
     def o_gather_of(p):

time: 54.7 us -> 54.8 us (level)
  no operation moved by 1% of the time
where the time goes in v5:
time: 54.8 us; the launch traced here: 54.7 us
  Pallas kernels  52.2 us (95%)
  local copies, waits for them, and re-layouts  1.89 us (3%)
  between operations  0.64 us (1%)
    pallas_call x1, Pallas kernels, local_step(): pl.pallas_call(lambda *refs: layer_kernel(tp_size, cp_size, *refs), out_s...  52.2 us
    unnamed x1, local copies, waits for them, and re-layouts  1.23 us

profile of v5, /device:TPU:97, one launch (start us, length us, event | category | flops | bytes accessed | tf_op | source)
XLA Modules:
  0.0 54.7 jit_solution(12749682823569547186)
XLA Ops:
  0.6 52.2 %layer.1 = (bf16[256,3584]{1,0:T(8,128)(2,1)S(1)}, bf16[2,256,128]{2,1,0:T(8,128)(2,1)S(1)}) custom-call(bf16[256,3584]{1,0:T(8,128)(2,1)} %refs_0_.1, s32[1,256]{1,0:T(1,128)} %bitcast.8, f32[28,128]{1,0:T(8,128)} %bitcast.7, bf16[3584,896]{1,0:T(8,128)(2,1)} %refs_3_.1, bf16[3584,128]{1,0:T(8,128)(2,1)} %refs_4_.1, bf16[3584,128]{1,0:T(8,128)(2,1)} %refs_5_.1, ...), custom_call_target="tpu_custom_call" | custom-call | tf_op jit(solution)/shard_map/layer/pallas_call | solution.py:518
  52.8 0.7 %slice_bitcast_fusion = (bf16[256,1,128]{2,0,1:T(8,128)(2,1)}, bf16[256,1,128]{2,0,1:T(8,128)(2,1)}) fusion(bf16[2,256,128]{2,1,0:T(8,128)(2,1)S(1)} %get-tuple-element.6), kind=kLoop, calls=%fused_computation | loop fusion | bytes 262144 | tf_op jit(solution)/shard_map/reshape;squeeze | solution.py:554
  53.5 1.2 %copy.12 = bf16[256,3584]{1,0:T(8,128)(2,1)} copy(bf16[256,3584]{1,0:T(8,128)(2,1)S(1)} %get-tuple-element.12) | data formatting | bytes 3670016
